TPU v7x, 128 devices: a whole 4x4x4 slice. The times are simulated.
128 devices in a mesh: problem: 1, samp: 16 (over z, y), feat: 8 (over x, core).
Axes of the slice: x: 4, y: 4, z: 4, core: 2. Of those that a mesh axis runs over, the one named last changes fastest.
Arguments:
- design: bfloat16 [8192, 65536], P(('problem', 'samp'), 'feat')
- targets: float32 [8192, 128], P(('problem', 'samp'))
- coef_init: float32 [65536, 128], P(('problem', 'feat'))
- step_sizes: float32 [65536], P(('problem', 'feat'))
- ridge_weights: float32 [128], P('problem')
Outputs:
- output 1: float32 [65536, 128], P(('problem', 'feat'))
- output 2: float32 [8192, 128], P(('problem', 'samp'))
All inputs are finite; a program needn't handle non-finite values.
Results may differ from a plain program's by a relative error of at most 0.00675681.
Values are sent between devices in bfloat16 or wider.
A program may use at most 1 GiB of HBM per device.

v0:
```python
import jax
import jax.numpy as jnp
from jax import lax
from jax.sharding import PartitionSpec as P

SWEEPS = 4
STEP_WEIGHT = 0.5


def solution(mesh):
    samp_size = mesh.shape["samp"]
    design_spec = P(("problem", "samp"), "feat")
    rows_spec = P(("problem", "samp"), None)
    coef_spec = P(("problem", "feat"), None)
    step_spec = P(("problem", "feat"))
    ridge_spec = P("problem")

    def local_sweeps(design, targets, coef_init, step_sizes, ridge_weights):
        total_rows = design.shape[0] * samp_size
        step_col = step_sizes[:, None]
        ridge_row = ridge_weights[None, :]

        def block_product(weights):
            product = jnp.dot(design, weights.astype(jnp.bfloat16), preferred_element_type=jnp.float32)
            return product.astype(jnp.bfloat16).astype(jnp.float32)

        resid_cur = targets - lax.psum(block_product(coef_init), "feat")
        coef_cur = coef_init
        for sweep_index in range(SWEEPS):
            part_grad = lax.dot_general(design, resid_cur.astype(jnp.bfloat16), (((0,), (0,)), ((), ())), preferred_element_type=jnp.float32)
            gradient = lax.psum(part_grad, "samp") / total_rows
            step_delta = step_col * (gradient - ridge_row * coef_cur)
            coef_cur = coef_cur + STEP_WEIGHT * step_delta
            resid_cur = resid_cur - STEP_WEIGHT * lax.psum(block_product(step_delta), "feat")
        return coef_cur, resid_cur

    return jax.shard_map(local_sweeps, mesh=mesh, in_specs=(design_spec, rows_spec, coef_spec, step_spec, ridge_spec), out_specs=(coef_spec, rows_spec), check_vma=False)
```

profile of v0, /device:TPU:1, one launch (start us, length us, event | category | flops | bytes accessed | tf_op | source)
XLA Modules:
  0.0 802.5 jit_solution(13405112412450391497)
XLA Ops:
  7.2 0.0 copy-start.3
  7.2 0.0 all-reduce.10.cloned.1.call-start
  7.2 7.6 fusion.29
  14.9 0.0 all-reduce.10.cloned.1.call-update
  14.9 0.0 all-reduce.12.cloned.1.call-start
  14.9 61.2 %all-reduce.10.cloned.1.call-done = f32[512,128]{1,0:T(8,128)} async-done(((f32[512,128]{1,0:T(8,128)}), f32[512,128]{1,0:T(8,128)}) %all-reduce.10.cloned.1.call-update) | async-done | bytes 262160 | tf_op jit(solution)/shard_map/psum | solution.py:27
  76.2 0.0 copy-done.3
  76.2 1.0 sub.27
  77.1 6.7 convolution_bitcast_fusion.3
  83.8 0.0 all-reduce.12.cloned.1.call-update
  83.9 0.0 copy-start
  83.9 0.0 copy-start.4
  83.9 0.0 all-reduce.14.cloned.1.call-start
  83.9 5.6 copy.8
  89.5 98.8 %all-reduce.12.cloned.1.call-done = f32[8192,128]{0,1:T(8,128)} async-done(((f32[8192,128]{0,1:T(8,128)}), f32[8192,128]{0,1:T(8,128)}) %all-reduce.12.cloned.1.call-update) | async-done | bytes 4194320 | tf_op jit(solution)/shard_map/psum | solution.py:31
  188.3 0.0 copy-done
  188.3 0.0 copy-done.4
  188.3 9.0 %fusion.38 = f32[512,128]{1,0:T(8,128)} fusion(bf16[512,8192]{1,0:T(8,128)(2,1)} %param.5, f32[8192,128]{0,1:T(8,128)} %copy.8, f32[8192,128]{0,1:T(8,128)} %all-reduce.12.cloned.1.call-done, f32[128]{0:T(128)S(1)} %copy-done.4, f32[8192]{0:T(1024)S(1)} %copy-done), kind=kOutput, calls=%fused_computation.38 | convolution fusion | flops 1079115776 | bytes 17072640 | tf_op jit(solution)/shard_map/dot_general | solution.py:24
  197.3 0.0 all-reduce.14.cloned.1.call-update
  197.3 0.0 all-reduce.16.cloned.1.call-start
  197.4 58.0 %all-reduce.14.cloned.1.call-done = f32[512,128]{1,0:T(8,128)} async-done(((f32[512,128]{1,0:T(8,128)}), f32[512,128]{1,0:T(8,128)}) %all-reduce.14.cloned.1.call-update) | async-done | bytes 262160 | tf_op jit(solution)/shard_map/psum | solution.py:34
  255.4 6.8 convolution_bitcast_fusion.2
  262.2 0.0 all-reduce.16.cloned.1.call-update
  262.2 0.0 copy-start.2
  262.3 0.0 all-reduce.18.cloned.1.call-start
  262.3 104.4 %all-reduce.16.cloned.1.call-done = f32[8192,128]{0,1:T(8,128)} async-done(((f32[8192,128]{0,1:T(8,128)}), f32[8192,128]{0,1:T(8,128)}) %all-reduce.16.cloned.1.call-update) | async-done | bytes 4194320 | tf_op jit(solution)/shard_map/psum | solution.py:31
  366.7 10.3 %fusion.47 = f32[512,128]{1,0:T(8,128)} fusion(bf16[512,8192]{1,0:T(8,128)(2,1)} %param.5, f32[8192,128]{0,1:T(8,128)} %all-reduce.16.cloned.1.call-done, f32[128]{0:T(128)S(1)} %copy-done.4, f32[8192]{0:T(1024)S(1)} %copy-done, f32[8192,128]{0,1:T(8,128)} %copy.8, f32[8192,128]{0,1:T(8,128)} %all-reduce.12.cloned.1.call-done), kind=kOutput, calls=%fused_computation.41 | convolution fusion | flops 1085407232 | bytes 21266944 | tf_op jit(solution)/shard_map/dot_general | solution.py:24
  377.0 0.0 all-reduce.18.cloned.1.call-update
  377.0 0.0 all-reduce.20.cloned.1.call-start
  377.1 58.1 %all-reduce.18.cloned.1.call-done = f32[512,128]{1,0:T(8,128)} async-done(((f32[512,128]{1,0:T(8,128)}), f32[512,128]{1,0:T(8,128)}) %all-reduce.18.cloned.1.call-update) | async-done | bytes 262160 | tf_op jit(solution)/shard_map/psum | solution.py:34
  435.2 0.0 copy-done.2
  435.2 1.0 multiply_subtract_fusion.2
  436.2 6.6 convolution_bitcast_fusion.1
  442.8 0.0 all-reduce.20.cloned.1.call-update
  442.9 0.2 all-reduce.22.cloned.1.call-start
  443.1 8.4 %multiply_add_fusion.2 = f32[8192,128]{0,1:T(8,128)} fusion(f32[8192,128]{0,1:T(8,128)} %all-reduce.16.cloned.1.call-done, f32[128]{0:T(128)S(1)} %copy-done.4, f32[8192]{0:T(1024)S(1)} %copy-done, f32[8192,128]{0,1:T(8,128)} %copy.8, f32[8192,128]{0,1:T(8,128)} %all-reduce.12.cloned.1.call-done), kind=kLoop, calls=%fused_computation.8 | loop fusion | flops 12582912 | bytes 16810496 | tf_op jit(solution)/shard_map/add | solution.py:33
  451.5 95.8 %all-reduce.20.cloned.1.call-done = f32[8192,128]{0,1:T(8,128)} async-done(((f32[8192,128]{0,1:T(8,128)}), f32[8192,128]{0,1:T(8,128)}) %all-reduce.20.cloned.1.call-update) | async-done | bytes 4194320 | tf_op jit(solution)/shard_map/psum | solution.py:31
  547.3 9.0 %fusion.56 = f32[512,128]{1,0:T(8,128)} fusion(bf16[512,8192]{1,0:T(8,128)(2,1)} %param.5, f32[8192,128]{0,1:T(8,128)} %multiply_add_fusion.2, f32[8192,128]{0,1:T(8,128)} %all-reduce.20.cloned.1.call-done, f32[128]{0:T(128)S(1)} %copy-done.4, f32[8192]{0:T(1024)S(1)} %copy-done), kind=kOutput, calls=%fused_computation.44 | convolution fusion | flops 1079115776 | bytes 17072640 | tf_op jit(solution)/shard_map/dot_general | solution.py:24
  556.3 0.0 all-reduce.22.cloned.1.call-update
  556.3 0.0 all-reduce.24.cloned.1.call-start
  556.4 58.1 %all-reduce.22.cloned.1.call-done = f32[512,128]{1,0:T(8,128)} async-done(((f32[512,128]{1,0:T(8,128)}), f32[512,128]{1,0:T(8,128)}) %all-reduce.22.cloned.1.call-update) | async-done | bytes 262160 | tf_op jit(solution)/shard_map/psum | solution.py:34
  614.5 6.8 convolution_bitcast_fusion
  621.2 0.0 all-reduce.24.cloned.1.call-update
  621.3 0.0 all-reduce.26.cloned.1.call-start
  621.3 104.4 %all-reduce.24.cloned.1.call-done = f32[8192,128]{0,1:T(8,128)} async-done(((f32[8192,128]{0,1:T(8,128)}), f32[8192,128]{0,1:T(8,128)}) %all-reduce.24.cloned.1.call-update) | async-done | bytes 4194320 | tf_op jit(solution)/shard_map/psum | solution.py:31
  725.7 10.3 %fusion.65 = f32[512,128]{1,0:T(8,128)} fusion(bf16[512,8192]{1,0:T(8,128)(2,1)} %param.5, f32[8192,128]{0,1:T(8,128)} %all-reduce.24.cloned.1.call-done, f32[128]{0:T(128)S(1)} %copy-done.4, f32[8192]{0:T(1024)S(1)} %copy-done, f32[8192,128]{0,1:T(8,128)} %multiply_add_fusion.2, f32[8192,128]{0,1:T(8,128)} %all-reduce.20.cloned.1.call-done), kind=kOutput, calls=%fused_computation.47 | convolution fusion | flops 1085407232 | bytes 21266944 | tf_op jit(solution)/shard_map/dot_general | solution.py:24
  736.0 0.0 all-reduce.26.cloned.1.call-update
  736.1 8.3 %multiply_add_fusion = f32[8192,128]{0,1:T(8,128)} fusion(f32[8192,128]{0,1:T(8,128)} %all-reduce.24.cloned.1.call-done, f32[128]{0:T(128)S(1)} %copy-done.4, f32[8192]{0:T(1024)S(1)} %copy-done, f32[8192,128]{0,1:T(8,128)} %multiply_add_fusion.2, f32[8192,128]{0,1:T(8,128)} %all-reduce.20.cloned.1.call-done), kind=kLoop, calls=%fused_computation.4 | loop fusion | flops 12582912 | bytes 16810496 | tf_op jit(solution)/shard_map/add | solution.py:33
  744.4 0.0 copy-start.1
  744.4 5.6 copy.13
  750.0 44.3 %all-reduce.26.cloned.1.call-done = f32[512,128]{1,0:T(8,128)} async-done(((f32[512,128]{1,0:T(8,128)}), f32[512,128]{1,0:T(8,128)}) %all-reduce.26.cloned.1.call-update) | async-done | bytes 262160 | tf_op jit(solution)/shard_map/psum | solution.py:34
  794.2 0.0 copy-done.1
  794.2 1.7 multiply_subtract_fusion
Async XLA Ops:
  7.2 69.0 %copy-start.3 = (f32[512,128]{1,0:T(8,128)S(1)}, f32[512,128]{1,0:T(8,128)}, u32[]{:S(2)}) copy-start(f32[512,128]{1,0:T(8,128)} %param.6) | copy-start | bytes 786436
  7.2 69.0 %all-reduce.10.cloned.1.call-start = ((), (), s32[]{:S(2)}) async-start(), calls=%async_computation | async-start | bytes 524288 | tf_op jit(solution)/shard_map/psum | solution.py:27
  14.9 173.4 %all-reduce.12.cloned.1.call-start = ((), (), s32[]{:S(2)}) async-start(), calls=%async_computation.1 | async-start | bytes 8388608 | tf_op jit(solution)/shard_map/psum | solution.py:31
  83.9 104.5 %copy-start = (f32[8192]{0:T(1024)S(1)}, f32[8192]{0:T(1024)}, u32[]{:S(2)}) copy-start(f32[8192]{0:T(1024)} %param.8) | copy-start | bytes 98308
  83.9 104.5 %copy-start.4 = (f32[128]{0:T(128)S(1)}, f32[128]{0:T(128)}, u32[]{:S(2)}) copy-start(f32[128]{0:T(128)} %param.9) | copy-start | bytes 1540
  83.9 171.6 %all-reduce.14.cloned.1.call-start = ((), (), s32[]{:S(2)}) async-start(), calls=%async_computation.2 | async-start | bytes 524288 | tf_op jit(solution)/shard_map/psum | solution.py:34
  197.3 169.3 %all-reduce.16.cloned.1.call-start = ((), (), s32[]{:S(2)}) async-start(), calls=%async_computation.3 | async-start | bytes 8388608 | tf_op jit(solution)/shard_map/psum | solution.py:31
  262.2 173.0 %copy-start.2 = (f32[512,128]{1,0:T(8,128)S(1)}, f32[512,128]{1,0:T(8,128)}, u32[]{:S(2)}) copy-start(f32[512,128]{1,0:T(8,128)} %all-reduce.14.cloned.1.call-done) | copy-start | bytes 786436
  262.3 172.9 %all-reduce.18.cloned.1.call-start = ((), (), s32[]{:S(2)}) async-start(), calls=%async_computation.4 | async-start | bytes 524288 | tf_op jit(solution)/shard_map/psum | solution.py:34
  377.0 170.3 %all-reduce.20.cloned.1.call-start = ((), (), s32[]{:S(2)}) async-start(), calls=%async_computation.5 | async-start | bytes 8388608 | tf_op jit(solution)/shard_map/psum | solution.py:31
  442.9 171.6 %all-reduce.22.cloned.1.call-start = ((), (), s32[]{:S(2)}) async-start(), calls=%async_computation.6 | async-start | bytes 524288 | tf_op jit(solution)/shard_map/psum | solution.py:34
  556.3 169.4 %all-reduce.24.cloned.1.call-start = ((), (), s32[]{:S(2)}) async-start(), calls=%async_computation.7 | async-start | bytes 8388608 | tf_op jit(solution)/shard_map/psum | solution.py:31
  621.3 173.0 %all-reduce.26.cloned.1.call-start = ((), (), s32[]{:S(2)}) async-start(), calls=%async_computation.8 | async-start | bytes 524288 | tf_op jit(solution)/shard_map/psum | solution.py:34
  744.4 49.9 %copy-start.1 = (f32[512,128]{1,0:T(8,128)S(1)}, f32[512,128]{1,0:T(8,128)}, u32[]{:S(2)}) copy-start(f32[512,128]{1,0:T(8,128)} %all-reduce.22.cloned.1.call-done) | copy-start | bytes 786436
Sparse Core Ops, SparseCore 0:
  15.0 61.1 all-reduce.9
  84.0 104.2 all-reduce.11
  197.5 57.9 all-reduce.13
  262.4 104.2 all-reduce.15
  377.2 57.9 all-reduce.17
  443.0 104.2 all-reduce.19
  556.4 57.9 all-reduce.21
  621.4 104.3 all-reduce.23
  736.2 57.9 all-reduce.25
where the time goes:
time: 804 us; the launch traced here: 802 us
  waiting for transfers between devices  683 us (85%)
  matrix products  73.1 us (9%)
  other arithmetic  20.3 us (3%)
  between operations  13.9 us (2%)
  local copies, waits for them, and re-layouts  11.2 us (1%)
    psum x4, waiting for transfers between devices, local_sweeps(): gradient = lax.psum(part_grad, 'samp') / total_rows  403 us
    psum x4, waiting for transfers between devices, local_sweeps(): lax.psum(block_product(step_delta), 'feat')  219 us
    psum x1, waiting for transfers between devices, local_sweeps(): resid_cur = targets - lax.psum(block_product(coef_init), 'feat')  61.2 us
    dot_general x5, matrix products, block_product(): jnp.dot(design, weights.astype(jnp.bfloat16), preferred_element_type=jnp....  46.3 us
    dot_general x4, matrix products, local_sweeps(): lax.dot_general(design, resid_cur.astype(jnp.bfloat16), (((0,), (0,)), ((...  26.9 us
    add x2, other arithmetic, local_sweeps(): coef_cur = coef_cur + STEP_WEIGHT * step_delta  16.7 us
  transfers between devices with their start and end apart: 9, of which 9 were waited for; matrix products, arithmetic and copies ran while one was open for 3% of the time, Pallas kernels for 0%

commit v1 on v0

v1 whole, which is shorter than its diff:
```python
import jax
import jax.numpy as jnp
from jax import lax
from jax.experimental import pallas as pl
from jax.experimental.pallas import tpu as pltpu
from jax.sharding import PartitionSpec as P

SWEEPS = 4
STEP_WEIGHT = 0.5
RING = 4
FEATS = 8
LANES = 128
ORDER = (2, 1, 3, 0)
STREAMS = 2
MESH_ID = pl.DeviceIdType.MESH
AG_MSGS = 22
F32 = jnp.float32
BF16 = jnp.bfloat16


def merge(first, second):
    live = [first, second]
    while live:
        for gen in list(live):
            try:
                next(gen)
            except StopIteration:
                live.remove(gen)


def run(gen):
    for _ in gen:
        pass


def make_kernel(total_rows, tgt):
    half = tgt // 2
    inv_rows = 1.0 / total_rows

    def kernel(x_hbm, y_hbm, w0_hbm, eta_ref, lam_ref, w_out, r_out,
               xv, wst, yst, sg, wg, gt, fin, din, cin, f2in, d2in, c2in, wown, lamb, rt, acc,
               ub, urecv, rbuf, rown, rfin,
               xsem, wsem, ysem, osem, rs_send, rs_recv, ag_recv, x_send, u_recv, r_recv, rf_recv):
        samp = lax.axis_index("samp")
        feat = lax.axis_index("feat")
        zpos = samp // RING
        ypos = samp % RING

        def wrap(v):
            return lax.rem(v + RING, RING)

        def dev(z, y):
            return (0, z * RING + y, feat)

        z_plus, z_minus = dev(wrap(zpos + 1), ypos), dev(wrap(zpos - 1), ypos)
        y_plus, y_minus = dev(zpos, wrap(ypos + 1)), dev(zpos, wrap(ypos - 1))
        first_nbr = ((y_plus, y_minus), (z_plus, z_minus))
        second_nbr = ((z_plus, z_minus), (y_plus, y_minus))

        def place(h, o1, o2):
            if h == 0:
                return wrap(zpos + o2), wrap(ypos + o1)
            return wrap(zpos + o1), wrap(ypos + o2)

        def peer(k):
            return lax.rem(feat + k, FEATS)

        x_copies = [pltpu.make_async_copy(x_hbm.at[:, pl.ds(c * 256, 256)], xv.at[c], xsem.at[c]) for c in range(32)]
        w_copies = [pltpu.make_async_copy(w0_hbm.at[pl.ds(8 * q, 8)], wst.at[pl.ds(8 * q, 8)], wsem.at[q]) for q in range(4)]
        y_copy = pltpu.make_async_copy(y_hbm.at[pl.ds(pl.multiple_of((feat // 2) * LANES, LANES), LANES)], yst, ysem)
        w_copies[0].start()
        y_copy.start()
        for q in range(4):
            if q:
                w_copies[q].start()
            for c in range(8 * q, 8 * q + 8):
                x_copies[c].start()

        barrier = pltpu.get_barrier_semaphore()
        for nbr in (z_plus, z_minus, y_plus, y_minus):
            pl.semaphore_signal(barrier, inc=1, device_id=nbr, device_id_type=MESH_ID)
        for k in range(1, FEATS):
            pl.semaphore_signal(barrier, inc=1, device_id=(0, samp, peer(k)), device_id_type=MESH_ID)
        pl.semaphore_wait(barrier, 4 + FEATS - 1)

        def remote(src, dst, send, recv, to):
            return pltpu.make_async_remote_copy(src_ref=src, dst_ref=dst, send_sem=send, recv_sem=recv, device_id=to, device_id_type=MESH_ID)

        def rs1(t, h, kind, way, jo):
            io, pm = {"F": (2, way), "D": (1 + 2 * way, 1 - way), "C": (1 + 2 * way, way)}[kind]
            land = {"F": fin, "D": din, "C": cin}[kind]
            slot = ((h * 3 + "FDC".index(kind)) * 2 + way) * 4 + jo
            return remote(gt.at[t, h, io, jo, pm], land.at[t, h, way, jo], rs_send.at[t, slot], rs_recv.at[t, slot], first_nbr[h][way])

        def rs2(t, h, kind, way):
            jo, pm = {"F": (2, way), "D": (1 + 2 * way, 1 - way), "C": (1 + 2 * way, way)}[kind]
            land = {"F": f2in, "D": d2in, "C": c2in}[kind]
            slot = 48 + (h * 3 + "FDC".index(kind)) * 2 + way
            return remote(gt.at[t, h, 0, jo, pm], land.at[t, h, way], rs_send.at[t, slot], rs_recv.at[t, slot], second_nbr[h][way])

        def ag(t, h, idx, buf, recv):
            if idx < 2:
                to, (o1, o2), rows = second_nbr[h][idx], (0, 0), None
            elif idx < 4:
                to, (o1, o2), rows = second_nbr[h][idx - 2], (0, (-1, 1)[idx - 2]), idx - 2
            elif idx < 14:
                way, m = (idx - 4) // 5, (idx - 4) % 5
                to, o1 = first_nbr[h][way], 0
                o2, rows = ((0, None), (-1, None), (1, None), (2, 0), (2, 1))[m]
            else:
                way, m = (idx - 14) // 4, (idx - 14) % 4
                to, o1, rows = first_nbr[h][way], (-1, 1)[way], way
                o2 = (0, -1, 1, 2)[m]
            zi, yi = place(h, o1, o2)
            ref = buf.at[t, zi, yi, h] if rows is None else buf.at[t, zi, yi, h, pl.ds(rows * half, half)]
            slot = h * AG_MSGS + idx
            return remote(ref, ref, rs_send.at[t, slot], recv.at[t, slot], to)

        def gather(t, buf, recv):
            def go(h, *idxs):
                for idx in idxs:
                    ag(t, h, idx, buf, recv).start()

            def got(h, *idxs):
                for idx in idxs:
                    ag(t, h, idx, buf, recv).wait_recv()

            for h in range(2):
                go(h, 0, 1, 4, 9)
            yield
            for h in range(2):
                got(h, 0)
                go(h, 2, 5, 10)
                got(h, 1)
                go(h, 3, 6, 11)
            yield
            for h in range(2):
                got(h, 4)
                go(h, 14)
                got(h, 9)
                go(h, 18)
            yield
            for h in range(2):
                got(h, 2)
                go(h, 7, 12)
                got(h, 3)
                go(h, 8, 13)
            yield
            for h in range(2):
                got(h, 5)
                go(h, 15)
                got(h, 6)
                go(h, 16)
                got(h, 10)
                go(h, 19)
                got(h, 11)
                go(h, 20)
            yield
            for h in range(2):
                got(h, 7)
                go(h, 17)
                got(h, 13)
                go(h, 21)
            yield
            for h in range(2):
                got(h, 8, 12, *range(14, 22))
            for h in range(2):
                for idx in range(AG_MSGS):
                    ag(t, h, idx, buf, recv).wait_send()

        def samp_phase(t):
            for io in ORDER:
                for h in range(2):
                    for jo in ORDER:
                        zi, yi = place(h, io, jo)
                        res = jnp.dot(rt[t], xv[(zi * RING + yi) * 2 + h], preferred_element_type=F32)
                        gt[t, h, io, jo, 0] = res[:, :LANES]
                        gt[t, h, io, jo, 1] = res[:, LANES:]
                        if io == 2:
                            rs1(t, h, "F", 0, jo).start()
                            rs1(t, h, "F", 1, jo).start()
                        elif io:
                            rs1(t, h, "D", io // 2, jo).start()
                yield
            for jo in ORDER:
                for h in range(2):
                    for way in range(2):
                        rs1(t, h, "F", way, jo).wait_recv()
                        gt[t, h, 1 + 2 * way, jo, way] += fin[t, h, way, jo]
                        rs1(t, h, "C", way, jo).start()
                yield
            for jo in ORDER:
                for h in range(2):
                    for way in range(2):
                        rs1(t, h, "D", way, jo).wait_recv()
                        rs1(t, h, "C", way, jo).wait_recv()
                    for pm in range(2):
                        gt[t, h, 0, jo, pm] = gt[t, h, 0, jo, pm] + cin[t, h, pm, jo] + din[t, h, 1 - pm, jo]
                    if jo == 2:
                        rs2(t, h, "F", 0).start()
                        rs2(t, h, "F", 1).start()
                    elif jo:
                        rs2(t, h, "D", jo // 2).start()
                yield
            for h in range(2):
                for way in range(2):
                    rs2(t, h, "F", way).wait_recv()
                    gt[t, h, 0, 1 + 2 * way, way] += f2in[t, h, way]
                    rs2(t, h, "C", way).start()
            yield
            for h in range(2):
                for way in range(2):
                    rs2(t, h, "D", way).wait_recv()
                    rs2(t, h, "C", way).wait_recv()
                for pm in range(2):
                    grad = (gt[t, h, 0, 0, pm] + c2in[t, h, pm] + d2in[t, h, 1 - pm]) * inv_rows
                    old = wown[t, h, pm]
                    step = eta_ref[pl.ds((samp * 2 + h) * 2 + pm, 1), :] * (grad - lamb[t] * old)
                    wown[t, h, pm] = old + STEP_WEIGHT * step
                    sg[t, zpos, ypos, h, :, pl.ds(pm * LANES, LANES)] = step.astype(BF16)
            for h in range(2):
                for kind in "FDC":
                    for way in range(2):
                        for jo in range(RING):
                            rs1(t, h, kind, way, jo).wait_send()
                        rs2(t, h, kind, way).wait_send()
            yield from gather(t, sg, ag_recv)

        def xmsg(t, k, src, dst, recv):
            return remote(src, dst, x_send.at[t, k], recv.at[t, k], (0, samp, peer(k)))

        def feat_phase(t, weight, loading=False, final=False):
            for zi in range(RING):
                part = None
                for yi in range(RING):
                    for h in range(2):
                        c = (zi * RING + yi) * 2 + h
                        if loading:
                            x_copies[c].wait()
                        prod = lax.dot_general(sg[t, zi, yi, h], xv[c], (((1,), (1,)), ((), ())), preferred_element_type=F32)
                        part = prod if part is None else part + prod
                acc[t] = part if zi == 0 else acc[t] + part
                yield
            for j in range(FEATS):
                ub[t, j] = acc[t, pl.ds((j % 2) * half, half), pl.ds((j // 2) * LANES, LANES)].astype(BF16)
            for k in range(1, FEATS):
                xmsg(t, k, ub.at[t, peer(k)], urecv.at[t, feat], u_recv).start()
            urecv[t, feat] = ub[t, feat]
            yield
            for k in range(1, FEATS):
                xmsg(t, k, ub.at[t, peer(k)], urecv.at[t, feat], u_recv).wait()
            total = urecv[t, 0].astype(F32)
            for j in range(1, FEATS):
                total = total + urecv[t, j].astype(F32)
            resid = rown[t] - weight * total
            rown[t] = resid
            if final:
                return
            rbuf[t, feat] = resid.astype(BF16)
            for k in range(1, FEATS):
                xmsg(t, k, rbuf.at[t, feat], rbuf.at[t, feat], r_recv).start()
            yield
            for k in range(1, FEATS):
                xmsg(t, k, rbuf.at[t, feat], rbuf.at[t, feat], r_recv).wait()
            for j in range(FEATS):
                rt[t, pl.ds((j % 2) * half, half), pl.ds((j // 2) * LANES, LANES)] = rbuf[t, j]
            yield

        lam_cols = jnp.broadcast_to(lam_ref[...], (LANES, LANES)).T
        for t in range(STREAMS):
            lamb[t] = lam_cols[t * tgt:(t + 1) * tgt]
        y_copy.wait()
        y_cols = yst[...].T
        core = lax.rem(feat, 2)
        yst[...] = y_cols
        for t in range(STREAMS):
            rown[t] = yst[pl.ds(pl.multiple_of(t * tgt + core * half, half), half), :]
        for q in range(4):
            w_copies[q].wait()

            def flip(c, carry, q=q):
                for pm in range(2):
                    cols = wst[8 * q + c, pl.ds(pm * LANES, LANES), :].T.astype(BF16)
                    for t in range(STREAMS):
                        sg[t, q, c // 2, lax.rem(c, 2), :, pl.ds(pm * LANES, LANES)] = cols[t * tgt:(t + 1) * tgt]
                return carry

            lax.fori_loop(0, 8, flip, 0)
        for h in range(2):
            for pm in range(2):
                cols = wst[samp * 2 + h, pl.ds(pm * LANES, LANES), :].T
                for t in range(STREAMS):
                    wown[t, h, pm] = cols[t * tgt:(t + 1) * tgt]

        run(feat_phase(0, 1.0, loading=True))

        def sweep(k, carry):
            weight = jnp.where(k == 0, 1.0, STEP_WEIGHT).astype(F32)
            merge(samp_phase(0), feat_phase(1, weight))
            merge(feat_phase(0, STEP_WEIGHT), samp_phase(1))
            return carry

        lax.fori_loop(0, SWEEPS, sweep, 0)

        def finish(t):
            for h in range(2):
                for pm in range(2):
                    wg[t, zpos, ypos, h, :, pl.ds(pm * LANES, LANES)] = wown[t, h, pm]
            yield from gather(t, wg, rs_recv)

        def rmsg(t, k):
            return xmsg(t, k, rfin.at[t, feat], rfin.at[t, feat], rf_recv)

        def residual():
            rfin[0, feat] = rown[0]
            for k in range(1, FEATS):
                rmsg(0, k).start()
            yield from feat_phase(1, STEP_WEIGHT, final=True)
            rfin[1, feat] = rown[1]
            for k in range(1, FEATS):
                rmsg(1, k).start()
            yield
            for t in range(STREAMS):
                for k in range(1, FEATS):
                    rmsg(t, k).wait()

        def both():
            merge_steps = [finish(0), finish(1)]
            while merge_steps:
                for gen in list(merge_steps):
                    try:
                        next(gen)
                    except StopIteration:
                        merge_steps.remove(gen)
                yield

        merge(both(), residual())
        w_done = pltpu.make_async_copy(wg, w_out, osem.at[0])
        r_done = pltpu.make_async_copy(rfin, r_out, osem.at[1])
        w_done.start()
        r_done.start()
        w_done.wait()
        r_done.wait()

    return kernel


def solution(mesh):
    samp_size = mesh.shape["samp"]
    design_spec = P(("problem", "samp"), "feat")
    rows_spec = P(("problem", "samp"), None)
    coef_spec = P(("problem", "feat"), None)
    step_spec = P(("problem", "feat"))
    ridge_spec = P("problem")

    def local(design, targets, coef_init, step_sizes, ridge_weights):
        rows, cols = design.shape
        n_tgt = targets.shape[1]
        tgt = n_tgt // STREAMS
        half = tgt // 2
        own = (STREAMS, RING, RING, 2, tgt, 256)
        vm = pltpu.VMEM
        dma = pltpu.SemaphoreType.DMA
        any_spec = pl.BlockSpec(memory_space=pl.ANY)
        vmem_spec = pl.BlockSpec(memory_space=pltpu.VMEM)
        w_t, r_t = pl.pallas_call(
            make_kernel(rows * samp_size, tgt),
            out_shape=(jax.ShapeDtypeStruct(own, F32), jax.ShapeDtypeStruct((STREAMS, FEATS, half, LANES), F32)),
            in_specs=[any_spec, any_spec, any_spec, vmem_spec, vmem_spec],
            out_specs=(any_spec, any_spec),
            scratch_shapes=[
                vm((32, rows, 256), BF16),
                vm((32, 256, LANES), F32),
                vm((LANES, LANES), F32),
                vm(own, BF16),
                vm(own, F32),
                vm((STREAMS, 2, RING, RING, 2, tgt, LANES), F32),
                vm((STREAMS, 2, 2, RING, tgt, LANES), F32),
                vm((STREAMS, 2, 2, RING, tgt, LANES), F32),
                vm((STREAMS, 2, 2, RING, tgt, LANES), F32),
                vm((STREAMS, 2, 2, tgt, LANES), F32),
                vm((STREAMS, 2, 2, tgt, LANES), F32),
                vm((STREAMS, 2, 2, tgt, LANES), F32),
                vm((STREAMS, 2, 2, tgt, LANES), F32),
                vm((STREAMS, tgt, LANES), F32),
                vm((STREAMS, tgt, rows), BF16),
                vm((STREAMS, tgt, rows), F32),
                vm((STREAMS, FEATS, half, LANES), BF16),
                vm((STREAMS, FEATS, half, LANES), BF16),
                vm((STREAMS, FEATS, half, LANES), BF16),
                vm((STREAMS, half, LANES), F32),
                vm((STREAMS, FEATS, half, LANES), F32),
                dma((32,)),
                dma((4,)),
                dma,
                dma((2,)),
                dma((STREAMS, 60)),
                dma((STREAMS, 60)),
                dma((STREAMS, 44)),
                dma((STREAMS, FEATS)),
                dma((STREAMS, FEATS)),
                dma((STREAMS, FEATS)),
                dma((STREAMS, FEATS)),
            ],
            compiler_params=pltpu.CompilerParams(collective_id=0, has_side_effects=True, vmem_limit_bytes=60 * 1024 * 1024),
        )(design, targets, coef_init.reshape(32, 256, n_tgt), step_sizes.reshape(cols // LANES, LANES), ridge_weights.reshape(1, n_tgt))
        coef = w_t.transpose(1, 2, 3, 5, 0, 4).reshape(cols, n_tgt)
        resid = r_t.reshape(STREAMS, RING, 2, half, LANES).transpose(1, 4, 0, 2, 3).reshape(rows, n_tgt)
        return coef, resid

    return jax.shard_map(local, mesh=mesh, in_specs=(design_spec, rows_spec, coef_spec, step_spec, ridge_spec), out_specs=(coef_spec, rows_spec), check_vma=False)
```

time: 804 us -> 378 us (0.47)
  waiting for transfers between devices: 683 us -> 0 us
  Pallas kernels: 0 us -> 354 us
  matrix products: 73.1 us -> 0 us
  other arithmetic: 20.3 us -> 0 us
  between operations: 13.9 us -> 0.65 us
  local copies, waits for them, and re-layouts: 11.2 us -> 22.9 us
    psum x9 -> x0, waiting for transfers between devices: 683 us -> none  [the longest x4 403 us: local_sweeps(): gradient = lax.psum(part_grad, 'samp') / total_rows]
    pallas_call x0 -> x1, Pallas kernels: none -> 354 us  [local(): pl.pallas_call(make_kernel(rows * samp_size, tgt), out_shape=(jax.ShapeDt...]
    dot_general x9 -> x0, matrix products: 73.1 us -> none  [the longest x5 46.3 us: block_product(): jnp.dot(design, weights.astype(jnp.bfloat16), preferred_element_type=jnp....]
    add x2 -> x0, other arithmetic: 16.7 us -> none  [local_sweeps(): coef_cur = coef_cur + STEP_WEIGHT * step_delta]
    unnamed x12 -> x4, local copies, waits for them, and re-layouts: 11.2 us -> 21.8 us
  transfers between devices with their start and end apart: 9 -> 0, of which waited for: 9 -> 0; matrix products, arithmetic and copies ran while one was open for 3% -> 0% of each run, Pallas kernels for 0% -> 0%
where the time goes in v1:
time: 378 us
  Pallas kernels  354 us (94%)
  local copies, waits for them, and re-layouts  22.9 us (6%)
    pallas_call x1, Pallas kernels, local(): pl.pallas_call(make_kernel(rows * samp_size, tgt), out_shape=(jax.ShapeDt...  354 us
    unnamed x4, local copies, waits for them, and re-layouts  21.8 us

profile of v1, /device:TPU:1, one launch (start us, length us, event | category | flops | bytes accessed | tf_op | source)
XLA Modules:
  0.0 377.6 jit_solution(13976801666250623729)
XLA Ops:
  0.6 354.0 %shard_map.68 = (f32[2,4,4,2,64,256]{5,4,3,2,1,0:T(8,128)}, f32[2,8,32,128]{3,2,1,0:T(8,128)}) custom-call(bf16[512,8192]{1,0:T(8,128)(2,1)} %x_hbm.1, f32[512,128]{1,0:T(8,128)} %y_hbm.1, f32[32,256,128]{2,1,0:T(8,128)} %bitcast.14, f32[64,128]{1,0:T(8,128)} %bitcast.18, f32[1,128]{1,0:T(1,128)} %bitcast.19), custom_call_target="tpu_custom_call" | custom-call | tf_op jit(solution)/shard_map/pallas_call | solution.py:366
  354.7 1.1 copy.9
  355.8 0.8 copy.11
  356.6 12.1 %copy.12 = f32[4,4,2,256,2,64]{5,4,3,2,1,0:T(2,128)} copy(f32[4,4,2,256,2,64]{3,5,2,1,0,4:T(8,128)} %bitcast.13) | data formatting | bytes 8388608
  368.8 8.8 %reshape.28 = f32[8192,128]{1,0:T(8,128)} reshape(f32[4,4,2,256,2,64]{5,4,3,2,1,0:T(2,128)} %copy.12) | data formatting | bytes 8388608
  (1 shorter events, 0.0 us)

commit v2 on v1

v2 whole, which is shorter than its diff:
```python
import jax
import jax.numpy as jnp
from jax import lax
from jax.experimental import pallas as pl
from jax.experimental.pallas import tpu as pltpu
from jax.sharding import PartitionSpec as P

SWEEPS = 4
STEP_WEIGHT = 0.5
RING = 4
FEATS = 8
LANES = 128
ORDER = (2, 1, 3, 0)
STREAMS = 2
MESH_ID = pl.DeviceIdType.MESH
AG_MSGS = 19
RS_MSGS = 26
FIRST = ""
ORDER_AB = "1"
ORDER_END = ""
F32 = jnp.float32
BF16 = jnp.bfloat16


def weave(order, *gens):
    live = dict(enumerate(gens))

    def step(i):
        if i in live:
            try:
                next(live[i])
            except StopIteration:
                del live[i]

    for ch in order:
        step(int(ch))
    while live:
        for i in sorted(live):
            step(i)


def run(gen):
    for _ in gen:
        pass


def make_kernel(total_rows, tgt):
    half = tgt // 2
    inv_rows = 1.0 / total_rows

    def kernel(x_hbm, y_hbm, w0_hbm, eta_ref, lam_ref, w_out, r_out,
               xv, wst, yst, rnat, flat, sg, wg, gt, fin, din, cin, r2in, wown, lamb, rt, acc,
               ub, urecv, rbuf, rown, rfin,
               xsem, wsem, ysem, rs_send, rs_recv, ag_recv, w_send, w_recv, x_send, u_recv, r_recv, rf_recv):
        samp = lax.axis_index("samp")
        feat = lax.axis_index("feat")
        zpos = samp // RING
        ypos = samp % RING

        def wrap(v):
            return lax.rem(v + RING, RING)

        def dev(z, y):
            return (0, z * RING + y, feat)

        z_plus, z_minus = dev(wrap(zpos + 1), ypos), dev(wrap(zpos - 1), ypos)
        y_plus, y_minus = dev(zpos, wrap(ypos + 1)), dev(zpos, wrap(ypos - 1))
        first_nbr = ((y_plus, y_minus), (z_plus, z_minus))
        second_nbr = ((z_plus, z_minus), (y_plus, y_minus))

        def place(h, o1, o2):
            if h == 0:
                return wrap(zpos + o2), wrap(ypos + o1)
            return wrap(zpos + o1), wrap(ypos + o2)

        def peer(k):
            return lax.rem(feat + k, FEATS)

        x_copies = [pltpu.make_async_copy(x_hbm.at[:, pl.ds(c * 256, 256)], xv.at[c], xsem.at[c]) for c in range(32)]
        w_copy = pltpu.make_async_copy(w0_hbm.at[pl.ds(samp * 2, 2)], wst.at[pl.ds(0, 2)], wsem.at[0])
        y_copy = pltpu.make_async_copy(y_hbm.at[pl.ds(pl.multiple_of((feat // 2) * LANES, LANES), LANES)], yst, ysem)
        w_copy.start()
        y_copy.start()
        for copy in x_copies:
            copy.start()

        barrier = pltpu.get_barrier_semaphore()
        for nbr in (z_plus, z_minus, y_plus, y_minus, dev(wrap(zpos + 2), ypos), dev(zpos, wrap(ypos + 2))):
            pl.semaphore_signal(barrier, inc=1, device_id=nbr, device_id_type=MESH_ID)
        for k in range(1, FEATS):
            pl.semaphore_signal(barrier, inc=1, device_id=(0, samp, peer(k)), device_id_type=MESH_ID)
        pl.semaphore_wait(barrier, 6 + FEATS - 1)

        def remote(src, dst, send, recv, to):
            return pltpu.make_async_remote_copy(src_ref=src, dst_ref=dst, send_sem=send, recv_sem=recv, device_id=to, device_id_type=MESH_ID)

        def rs1(t, h, kind, way, part):
            io, pm = {"F": (2, way), "D": (1 + 2 * way, 1 - way), "C": (1 + 2 * way, way)}[kind]
            land = {"F": fin, "D": din, "C": cin}[kind]
            rows = pl.ds(0, 4) if kind == "D" else pl.ds(2 * part, 2)
            slot = (h * 2 + way) * 5 + {"F": part, "C": 2 + part, "D": 4}[kind]
            return remote(gt.at[t, h, io, pm, rows], land.at[t, h, way, rows], rs_send.at[t, slot], rs_recv.at[t, slot], first_nbr[h][way])

        def rs2(t, h, js):
            jo = ORDER[js]
            slot = 20 + h * 3 + js
            zi, yi = place(h, 0, jo)
            return remote(gt.at[t, h, 0, :, js], r2in.at[t, h, js], rs_send.at[t, slot], rs_recv.at[t, slot], dev(zi, yi))

        def ag(t, h, idx, buf, send, recv):
            if idx < 3:
                (o1, o2), rows = (0, 0), None
                to = dev(*place(h, 0, ORDER[idx]))
            elif idx < 11:
                way, m = (idx - 3) // 4, (idx - 3) % 4
                to, o1, rows = first_nbr[h][way], 0, None
                o2 = (0, -1, 1, 2)[m]
            else:
                way, m = (idx - 11) // 4, (idx - 11) % 4
                to, o1, rows = first_nbr[h][way], (-1, 1)[way], way
                o2 = (0, -1, 1, 2)[m]
            zi, yi = place(h, o1, o2)
            ref = buf.at[t, zi, yi, h] if rows is None else buf.at[t, zi, yi, h, pl.ds(rows * half, half)]
            slot = h * AG_MSGS + idx
            return remote(ref, ref, send.at[t, slot], recv.at[t, slot], to)

        def gather(t, buf, send, recv, work=None):
            def go(h, *idxs):
                for idx in idxs:
                    ag(t, h, idx, buf, send, recv).start()

            def got(h, *idxs):
                for idx in idxs:
                    ag(t, h, idx, buf, send, recv).wait_recv()

            for h in range(2):
                go(h, 0, 1, 2, 3, 7)
            yield
            for h in range(2):
                got(h, 1)
                go(h, 4, 8)
                got(h, 2)
                go(h, 5, 9)
                got(h, 0)
                go(h, 6, 10)
            yield
            if work:
                work(0)
                yield
            for h in range(2):
                got(h, 3)
                go(h, 11)
                got(h, 7)
                go(h, 15)
            yield
            for h in range(2):
                for m in range(1, 4):
                    got(h, 3 + m)
                    go(h, 11 + m)
                    got(h, 7 + m)
                    go(h, 15 + m)
            yield
            if work:
                work(-1)
                yield
                work(1)
                yield
            for h in range(2):
                got(h, *range(11, 19))
            if work:
                work(2)
            for h in range(2):
                for idx in range(AG_MSGS):
                    ag(t, h, idx, buf, send, recv).wait_send()

        def samp_phase(t):
            for io in ORDER:
                for h in range(2):
                    for js in range(RING):
                        zi, yi = place(h, io, ORDER[js])
                        res = jnp.dot(rt[t], xv[(zi * RING + yi) * 2 + h], preferred_element_type=F32)
                        gt[t, h, io, 0, js] = res[:, :LANES]
                        gt[t, h, io, 1, js] = res[:, LANES:]
                        if io == 2 and js % 2:
                            rs1(t, h, "F", 0, js // 2).start()
                            rs1(t, h, "F", 1, js // 2).start()
                    if io % 2:
                        rs1(t, h, "D", io // 2, 0).start()
                yield
            for part in range(2):
                rows = pl.ds(2 * part, 2)
                for h in range(2):
                    for way in range(2):
                        rs1(t, h, "F", way, part).wait_recv()
                        gt[t, h, 1 + 2 * way, way, rows] += fin[t, h, way, rows]
                        rs1(t, h, "C", way, part).start()
                yield
            for part in range(2):
                for h in range(2):
                    for way in range(2):
                        if part == 0:
                            rs1(t, h, "D", way, 0).wait_recv()
                        rs1(t, h, "C", way, part).wait_recv()
                    for js in range(2 * part, 2 * part + 2):
                        for pm in range(2):
                            gt[t, h, 0, pm, js] = gt[t, h, 0, pm, js] + cin[t, h, pm, js] + din[t, h, 1 - pm, js]
                        if js < 3:
                            rs2(t, h, js).start()
                yield
            for h in range(2):
                for js in range(3):
                    rs2(t, h, js).wait_recv()
                for pm in range(2):
                    grad = (gt[t, h, 0, pm, 3] + r2in[t, h, 0, pm] + r2in[t, h, 1, pm] + r2in[t, h, 2, pm]) * inv_rows
                    old = wown[t, h, pm]
                    step = eta_ref[pl.ds((samp * 2 + h) * 2 + pm, 1), :] * (grad - lamb[t] * old)
                    wown[t, h, pm] = old + STEP_WEIGHT * step
                    sg[t, zpos, ypos, h, :, pl.ds(pm * LANES, LANES)] = step.astype(BF16)
            for h in range(2):
                for way in range(2):
                    rs1(t, h, "D", way, 0).wait_send()
                    for part in range(2):
                        rs1(t, h, "F", way, part).wait_send()
                        rs1(t, h, "C", way, part).wait_send()
                for js in range(3):
                    rs2(t, h, js).wait_send()

        def xmsg(t, k, src, dst, recv):
            return remote(src, dst, x_send.at[t, k], recv.at[t, k], (0, samp, peer(k)))

        def feat_phase(t, weight, loading=False, final=False):
            def work(o1):
                if loading and o1 == 0:
                    for copy in x_copies:
                        copy.wait()
                part = None
                for h in range(2):
                    for o2 in (0, -1, 1, 2):
                        zi, yi = place(h, o1, o2)
                        c = (zi * RING + yi) * 2 + h
                        prod = lax.dot_general(sg[t, zi, yi, h], xv[c], (((1,), (1,)), ((), ())), preferred_element_type=F32)
                        part = prod if part is None else part + prod
                acc[t] = part if o1 == 0 else acc[t] + part

            yield from gather(t, sg, rs_send, ag_recv, work)
            for j in range(FEATS):
                ub[t, j] = acc[t, pl.ds((j % 2) * half, half), pl.ds((j // 2) * LANES, LANES)].astype(BF16)
            for k in range(1, FEATS):
                xmsg(t, k, ub.at[t, peer(k)], urecv.at[t, feat], u_recv).start()
            urecv[t, feat] = ub[t, feat]
            yield
            for k in range(1, FEATS):
                xmsg(t, k, ub.at[t, peer(k)], urecv.at[t, feat], u_recv).wait()
            total = urecv[t, 0].astype(F32)
            for j in range(1, FEATS):
                total = total + urecv[t, j].astype(F32)
            resid = rown[t] - weight * total
            rown[t] = resid
            if final:
                return
            rbuf[t, feat] = resid.astype(BF16)
            for k in range(1, FEATS):
                xmsg(t, k, rbuf.at[t, feat], rbuf.at[t, feat], r_recv).start()
            yield
            for k in range(1, FEATS):
                xmsg(t, k, rbuf.at[t, feat], rbuf.at[t, feat], r_recv).wait()
            for j in range(FEATS):
                rt[t, pl.ds((j % 2) * half, half), pl.ds((j // 2) * LANES, LANES)] = rbuf[t, j]
            yield

        lam_cols = jnp.broadcast_to(lam_ref[...], (LANES, LANES)).T
        for t in range(STREAMS):
            lamb[t] = lam_cols[t * tgt:(t + 1) * tgt]
        y_copy.wait()
        y_cols = yst[...].T
        core = lax.rem(feat, 2)
        yst[...] = y_cols
        for t in range(STREAMS):
            rown[t] = yst[pl.ds(pl.multiple_of(t * tgt + core * half, half), half), :]
        w_copy.wait()
        for h in range(2):
            for pm in range(2):
                cols = wst[h, pl.ds(pm * LANES, LANES), :].T
                for t in range(STREAMS):
                    mine = cols[t * tgt:(t + 1) * tgt]
                    wown[t, h, pm] = mine
                    sg[t, zpos, ypos, h, :, pl.ds(pm * LANES, LANES)] = mine.astype(BF16)

        run(feat_phase(0, 1.0, loading=True))

        def sweep(k, carry):
            weight = jnp.where(k == 0, 1.0, STEP_WEIGHT).astype(F32)
            weave(ORDER_AB, samp_phase(0), feat_phase(1, weight))
            weave(ORDER_AB, samp_phase(1), feat_phase(0, STEP_WEIGHT))
            return carry

        lax.fori_loop(0, SWEEPS, sweep, 0)

        def coef_out(t):
            for h in range(2):
                for pm in range(2):
                    wg[t, zpos, ypos, h, :, pl.ds(pm * LANES, LANES)] = wown[t, h, pm]
            yield from gather(t, wg, w_send, w_recv)

        def rmsg(t, k):
            return xmsg(t, k, rfin.at[t, feat], rfin.at[t, feat], rf_recv)

        def last(t):
            yield from feat_phase(t, STEP_WEIGHT, final=True)
            rfin[t, feat] = rown[t]
            for k in range(1, FEATS):
                rmsg(t, k).start()
            yield
            for k in range(1, FEATS):
                rmsg(t, k).wait()

        rfin[0, feat] = rown[0]
        for k in range(1, FEATS):
            rmsg(0, k).start()
        weave(ORDER_END, last(1), coef_out(0), coef_out(1))
        for k in range(1, FEATS):
            rmsg(0, k).wait()

        for q in range(4):
            def flop(c, carry, q=q):
                for pm in range(2):
                    for t in range(STREAMS):
                        flat[pm, t * tgt:(t + 1) * tgt] = wg[t, q, c // 2, lax.rem(c, 2), :, pl.ds(pm * LANES, LANES)]
                for pm in range(2):
                    wst[8 * q + c, pl.ds(pm * LANES, LANES), :] = flat[pm].T
                return carry

            lax.fori_loop(0, 8, flop, 0)
            pltpu.make_async_copy(wst.at[pl.ds(8 * q, 8)], w_out.at[pl.ds(8 * q, 8)], wsem.at[q]).start()
        for xc in range(4):
            for t in range(STREAMS):
                for core_id in range(2):
                    flat[xc % 2, pl.ds(t * tgt + core_id * half, half), :] = rfin[t, 2 * xc + core_id]
            rnat[xc] = flat[xc % 2].T
        r_done = pltpu.make_async_copy(rnat, r_out, ysem)
        r_done.start()
        for q in range(4):
            pltpu.make_async_copy(wst.at[pl.ds(8 * q, 8)], w_out.at[pl.ds(8 * q, 8)], wsem.at[q]).wait()
        r_done.wait()

    return kernel


def solution(mesh):
    samp_size = mesh.shape["samp"]
    design_spec = P(("problem", "samp"), "feat")
    rows_spec = P(("problem", "samp"), None)
    coef_spec = P(("problem", "feat"), None)
    step_spec = P(("problem", "feat"))
    ridge_spec = P("problem")

    def local(design, targets, coef_init, step_sizes, ridge_weights):
        rows, cols = design.shape
        n_tgt = targets.shape[1]
        tgt = n_tgt // STREAMS
        half = tgt // 2
        own = (STREAMS, RING, RING, 2, tgt, 256)
        vm = pltpu.VMEM
        dma = pltpu.SemaphoreType.DMA
        any_spec = pl.BlockSpec(memory_space=pl.ANY)
        vmem_spec = pl.BlockSpec(memory_space=pltpu.VMEM)
        w_t, r_t = pl.pallas_call(
            make_kernel(rows * samp_size, tgt),
            out_shape=(jax.ShapeDtypeStruct((32, 256, n_tgt), F32), jax.ShapeDtypeStruct((rows // LANES, LANES, n_tgt), F32)),
            in_specs=[any_spec, any_spec, any_spec, vmem_spec, vmem_spec],
            out_specs=(any_spec, any_spec),
            scratch_shapes=[
                vm((32, rows, 256), BF16),
                vm((32, 256, LANES), F32),
                vm((LANES, LANES), F32),
                vm((rows // LANES, LANES, n_tgt), F32),
                vm((2, LANES, n_tgt), F32),
                vm(own, BF16),
                vm(own, F32),
                vm((STREAMS, 2, RING, 2, RING, tgt, LANES), F32),
                vm((STREAMS, 2, 2, RING, tgt, LANES), F32),
                vm((STREAMS, 2, 2, RING, tgt, LANES), F32),
                vm((STREAMS, 2, 2, RING, tgt, LANES), F32),
                vm((STREAMS, 2, 3, 2, tgt, LANES), F32),
                vm((STREAMS, 2, 2, tgt, LANES), F32),
                vm((STREAMS, tgt, LANES), F32),
                vm((STREAMS, tgt, rows), BF16),
                vm((STREAMS, tgt, rows), F32),
                vm((STREAMS, FEATS, half, LANES), BF16),
                vm((STREAMS, FEATS, half, LANES), BF16),
                vm((STREAMS, FEATS, half, LANES), BF16),
                vm((STREAMS, half, LANES), F32),
                vm((STREAMS, FEATS, half, LANES), F32),
                dma((32,)),
                dma((4,)),
                dma,
                dma((STREAMS, 2 * AG_MSGS)),
                dma((STREAMS, RS_MSGS)),
                dma((STREAMS, 2 * AG_MSGS)),
                dma((STREAMS, 2 * AG_MSGS)),
                dma((STREAMS, 2 * AG_MSGS)),
                dma((STREAMS, FEATS)),
                dma((STREAMS, FEATS)),
                dma((STREAMS, FEATS)),
                dma((STREAMS, FEATS)),
            ],
            compiler_params=pltpu.CompilerParams(collective_id=0, has_side_effects=True, vmem_limit_bytes=60 * 1024 * 1024),
        )(design, targets, coef_init.reshape(32, 256, n_tgt), step_sizes.reshape(cols // LANES, LANES), ridge_weights.reshape(1, n_tgt))
        coef = w_t.reshape(cols, n_tgt)
        resid = r_t.reshape(rows, n_tgt)
        return coef, resid

    return jax.shard_map(local, mesh=mesh, in_specs=(design_spec, rows_spec, coef_spec, step_spec, ridge_spec), out_specs=(coef_spec, rows_spec), check_vma=False)
```

time: 378 us -> 275 us (0.73)
  Pallas kernels: 354 us -> 269 us
  local copies, waits for them, and re-layouts: 22.9 us -> 5.22 us
    pallas_call x1, Pallas kernels: 354 us -> 269 us  [local(): pl.pallas_call(make_kernel(rows * samp_size, tgt), out_shape=(jax.ShapeDt...]
    unnamed x4, local copies, waits for them, and re-layouts: 21.8 us -> 5.22 us
where the time goes in v2:
time: 275 us
  Pallas kernels  269 us (98%)
  local copies, waits for them, and re-layouts  5.22 us (2%)
    pallas_call x1, Pallas kernels, local(): pl.pallas_call(make_kernel(rows * samp_size, tgt), out_shape=(jax.ShapeDt...  269 us

profile of v2, /device:TPU:1, one launch (start us, length us, event | category | flops | bytes accessed | tf_op | source)
XLA Modules:
  0.0 274.6 jit_solution(11764485620355306560)
XLA Ops:
  0.6 268.7 %shard_map.68 = (f32[32,256,128]{2,1,0:T(8,128)}, f32[4,128,128]{2,1,0:T(8,128)}) custom-call(bf16[512,8192]{1,0:T(8,128)(2,1)} %x_hbm.1, f32[512,128]{1,0:T(8,128)} %y_hbm.1, f32[32,256,128]{2,1,0:T(8,128)} %bitcast.5, f32[64,128]{1,0:T(8,128)} %bitcast.8, f32[1,128]{1,0:T(1,128)} %bitcast.9), custom_call_target="tpu_custom_call" | custom-call | tf_op jit(solution)/shard_map/pallas_call | solution.py:367
  269.4 0.0 copy-start
  269.4 4.5 %copy.9 = f32[8192,128]{1,0:T(8,128)} copy(f32[8192,128]{1,0:T(8,128)} %bitcast.6) | data formatting | bytes 8388608
  273.9 0.0 copy-done
  273.9 0.7 copy.10
Async XLA Ops:
  269.4 4.5 %copy-start = (f32[4,128,128]{2,1,0:T(8,128)S(1)}, f32[4,128,128]{2,1,0:T(8,128)}, u32[]{:S(2)}) copy-start(f32[4,128,128]{2,1,0:T(8,128)} %get-tuple-element.5) | copy-start | bytes 786436

commit v3 on v2

--- a/solution.py
+++ b/solution.py
@@ -11,37 +11,12 @@
 FEATS = 8
 LANES = 128
 ORDER = (2, 1, 3, 0)
-STREAMS = 2
+STREAMS = 4
 MESH_ID = pl.DeviceIdType.MESH
 AG_MSGS = 19
 RS_MSGS = 26
-FIRST = ""
-ORDER_AB = "1"
-ORDER_END = ""
 F32 = jnp.float32
 BF16 = jnp.bfloat16
-
-
-def weave(order, *gens):
-    live = dict(enumerate(gens))
-
-    def step(i):
-        if i in live:
-            try:
-                next(live[i])
-            except StopIteration:
-                del live[i]
-
-    for ch in order:
-        step(int(ch))
-    while live:
-        for i in sorted(live):
-            step(i)
-
-
-def run(gen):
-    for _ in gen:
-        pass
 
 
 def make_kernel(total_rows, tgt):
@@ -124,69 +99,65 @@
             slot = h * AG_MSGS + idx
             return remote(ref, ref, send.at[t, slot], recv.at[t, slot], to)
 
-        def gather(t, buf, send, recv, work=None):
-            def go(h, *idxs):
-                for idx in idxs:
-                    ag(t, h, idx, buf, send, recv).start()
-
-            def got(h, *idxs):
-                for idx in idxs:
-                    ag(t, h, idx, buf, send, recv).wait_recv()
-
-            for h in range(2):
-                go(h, 0, 1, 2, 3, 7)
-            yield
-            for h in range(2):
-                got(h, 1)
-                go(h, 4, 8)
-                got(h, 2)
-                go(h, 5, 9)
-                got(h, 0)
-                go(h, 6, 10)
-            yield
-            if work:
-                work(0)
-                yield
-            for h in range(2):
-                got(h, 3)
-                go(h, 11)
-                got(h, 7)
-                go(h, 15)
-            yield
+        def go(t, h, net, *idxs):
+            for idx in idxs:
+                ag(t, h, idx, *net).start()
+
+        def got(t, h, net, *idxs):
+            for idx in idxs:
+                ag(t, h, idx, *net).wait_recv()
+
+        step_net = (sg, rs_send, ag_recv)
+        coef_net = (wg, w_send, w_recv)
+
+        def gather_open(t, net):
+            for h in range(2):
+                go(t, h, net, 1, 2, 0, 3, 7)
+
+        def gather_second(t, net):
+            for h in range(2):
+                got(t, h, net, 1)
+                go(t, h, net, 4, 8)
+                got(t, h, net, 2)
+                go(t, h, net, 5, 9)
+            for h in range(2):
+                got(t, h, net, 0)
+                go(t, h, net, 6, 10)
+            for h in range(2):
+                got(t, h, net, 3)
+                go(t, h, net, 11)
+                got(t, h, net, 7)
+                go(t, h, net, 15)
+
+        def gather_third(t, net):
             for h in range(2):
                 for m in range(1, 4):
-                    got(h, 3 + m)
-                    go(h, 11 + m)
-                    got(h, 7 + m)
-                    go(h, 15 + m)
-            yield
-            if work:
-                work(-1)
-                yield
-                work(1)
-                yield
-            for h in range(2):
-                got(h, *range(11, 19))
-            if work:
-                work(2)
+                    got(t, h, net, 3 + m)
+                    go(t, h, net, 11 + m)
+                    got(t, h, net, 7 + m)
+                    go(t, h, net, 15 + m)
+
+        def gather_close(t, net):
+            for h in range(2):
+                got(t, h, net, *range(11, 19))
             for h in range(2):
                 for idx in range(AG_MSGS):
-                    ag(t, h, idx, buf, send, recv).wait_send()
-
-        def samp_phase(t):
-            for io in ORDER:
-                for h in range(2):
-                    for js in range(RING):
-                        zi, yi = place(h, io, ORDER[js])
-                        res = jnp.dot(rt[t], xv[(zi * RING + yi) * 2 + h], preferred_element_type=F32)
-                        gt[t, h, io, 0, js] = res[:, :LANES]
-                        gt[t, h, io, 1, js] = res[:, LANES:]
-                        if io == 2 and js % 2:
-                            rs1(t, h, "F", 0, js // 2).start()
-                            rs1(t, h, "F", 1, js // 2).start()
-                    if io % 2:
-                        rs1(t, h, "D", io // 2, 0).start()
-                yield
+                    ag(t, h, idx, *net).wait_send()
+
+        def slopes(t, io):
+            for h in range(2):
+                for js in range(RING):
+                    zi, yi = place(h, io, ORDER[js])
+                    res = jnp.dot(rt[t], xv[(zi * RING + yi) * 2 + h], preferred_element_type=F32)
+                    gt[t, h, io, 0, js] = res[:, :LANES]
+                    gt[t, h, io, 1, js] = res[:, LANES:]
+                    if io == 2 and js % 2:
+                        rs1(t, h, "F", 0, js // 2).start()
+                        rs1(t, h, "F", 1, js // 2).start()
+                if io % 2:
+                    rs1(t, h, "D", io // 2, 0).start()
+
+        def sum_first(t):
             for part in range(2):
                 rows = pl.ds(2 * part, 2)
                 for h in range(2):
@@ -194,7 +165,8 @@
                         rs1(t, h, "F", way, part).wait_recv()
                         gt[t, h, 1 + 2 * way, way, rows] += fin[t, h, way, rows]
                         rs1(t, h, "C", way, part).start()
-                yield
+
+        def sum_second(t):
             for part in range(2):
                 for h in range(2):
                     for way in range(2):
@@ -206,7 +178,8 @@
                             gt[t, h, 0, pm, js] = gt[t, h, 0, pm, js] + cin[t, h, pm, js] + din[t, h, 1 - pm, js]
                         if js < 3:
                             rs2(t, h, js).start()
-                yield
+
+        def take_step(t):
             for h in range(2):
                 for js in range(3):
                     rs2(t, h, js).wait_recv()
@@ -225,48 +198,64 @@
                 for js in range(3):
                     rs2(t, h, js).wait_send()
 
+        def coef_open(t):
+            for h in range(2):
+                for pm in range(2):
+                    wg[t, zpos, ypos, h, :, pl.ds(pm * LANES, LANES)] = wown[t, h, pm]
+            gather_open(t, coef_net)
+
+        def products(t, o1):
+            part = None
+            for h in range(2):
+                for o2 in (0, -1, 1, 2):
+                    zi, yi = place(h, o1, o2)
+                    c = (zi * RING + yi) * 2 + h
+                    prod = lax.dot_general(sg[t, zi, yi, h], xv[c], (((1,), (1,)), ((), ())), preferred_element_type=F32)
+                    part = prod if part is None else part + prod
+            acc[t] = part if o1 == 0 else acc[t] + part
+
         def xmsg(t, k, src, dst, recv):
             return remote(src, dst, x_send.at[t, k], recv.at[t, k], (0, samp, peer(k)))
 
-        def feat_phase(t, weight, loading=False, final=False):
-            def work(o1):
-                if loading and o1 == 0:
-                    for copy in x_copies:
-                        copy.wait()
-                part = None
-                for h in range(2):
-                    for o2 in (0, -1, 1, 2):
-                        zi, yi = place(h, o1, o2)
-                        c = (zi * RING + yi) * 2 + h
-                        prod = lax.dot_general(sg[t, zi, yi, h], xv[c], (((1,), (1,)), ((), ())), preferred_element_type=F32)
-                        part = prod if part is None else part + prod
-                acc[t] = part if o1 == 0 else acc[t] + part
-
-            yield from gather(t, sg, rs_send, ag_recv, work)
+        def umsg(t, k):
+            return xmsg(t, k, ub.at[t, peer(k)], urecv.at[t, feat], u_recv)
+
+        def rmsg(t, k):
+            return xmsg(t, k, rbuf.at[t, feat], rbuf.at[t, feat], r_recv)
+
+        def fmsg(t, k):
+            return xmsg(t, k, rfin.at[t, feat], rfin.at[t, feat], rf_recv)
+
+        def blocks_out(t):
             for j in range(FEATS):
                 ub[t, j] = acc[t, pl.ds((j % 2) * half, half), pl.ds((j // 2) * LANES, LANES)].astype(BF16)
             for k in range(1, FEATS):
-                xmsg(t, k, ub.at[t, peer(k)], urecv.at[t, feat], u_recv).start()
+                umsg(t, k).start()
             urecv[t, feat] = ub[t, feat]
-            yield
-            for k in range(1, FEATS):
-                xmsg(t, k, ub.at[t, peer(k)], urecv.at[t, feat], u_recv).wait()
+
+        def residual(t, weight):
+            for k in range(1, FEATS):
+                umsg(t, k).wait()
             total = urecv[t, 0].astype(F32)
             for j in range(1, FEATS):
                 total = total + urecv[t, j].astype(F32)
-            resid = rown[t] - weight * total
-            rown[t] = resid
-            if final:
-                return
-            rbuf[t, feat] = resid.astype(BF16)
-            for k in range(1, FEATS):
-                xmsg(t, k, rbuf.at[t, feat], rbuf.at[t, feat], r_recv).start()
-            yield
-            for k in range(1, FEATS):
-                xmsg(t, k, rbuf.at[t, feat], rbuf.at[t, feat], r_recv).wait()
+            rown[t] = rown[t] - weight * total
+
+        def residual_out(t):
+            rbuf[t, feat] = rown[t].astype(BF16)
+            for k in range(1, FEATS):
+                rmsg(t, k).start()
+
+        def residual_final(t):
+            rfin[t, feat] = rown[t]
+            for k in range(1, FEATS):
+                fmsg(t, k).start()
+
+        def residual_in(t):
+            for k in range(1, FEATS):
+                rmsg(t, k).wait()
             for j in range(FEATS):
                 rt[t, pl.ds((j % 2) * half, half), pl.ds((j // 2) * LANES, LANES)] = rbuf[t, j]
-            yield
 
         lam_cols = jnp.broadcast_to(lam_ref[...], (LANES, LANES)).T
         for t in range(STREAMS):
@@ -286,40 +275,102 @@
                     wown[t, h, pm] = mine
                     sg[t, zpos, ypos, h, :, pl.ds(pm * LANES, LANES)] = mine.astype(BF16)
 
-        run(feat_phase(0, 1.0, loading=True))
-
-        def sweep(k, carry):
-            weight = jnp.where(k == 0, 1.0, STEP_WEIGHT).astype(F32)
-            weave(ORDER_AB, samp_phase(0), feat_phase(1, weight))
-            weave(ORDER_AB, samp_phase(1), feat_phase(0, STEP_WEIGHT))
+        for t in range(STREAMS):
+            gather_open(t, step_net)
+        for copy in x_copies:
+            copy.wait()
+
+        rounds = STREAMS * SWEEPS
+
+        def one_pass(i, carry):
+            ta, tb, tc, td = (lax.rem(i + off, STREAMS) for off in (2, 1, 0, 3))
+            in_a = (i >= 2) & (i < 2 + rounds)
+            in_b = (i >= 3) & (i < 3 + rounds)
+            in_c = i < STREAMS + rounds
+            in_d = i >= 1
+            wrap_up = i >= 3 + rounds - STREAMS
+            ending = i >= 1 + rounds
+            weight = jnp.where(i <= STREAMS, 1.0, STEP_WEIGHT).astype(F32)
+
+            @pl.when(in_a)
+            def _():
+                residual_in(ta)
+                slopes(ta, 2)
+
+            @pl.when(in_b)
+            def _():
+                sum_second(tb)
+
+            @pl.when(in_d)
+            def _():
+                gather_close(td, step_net)
+                products(td, 2)
+                blocks_out(td)
+
+            @pl.when(in_c)
+            def _():
+                gather_second(tc, step_net)
+
+            @pl.when(in_a)
+            def _():
+                slopes(ta, 1)
+                slopes(ta, 3)
+                slopes(ta, 0)
+
+            @pl.when(in_a)
+            def _():
+                sum_first(ta)
+
+            @pl.when(in_d)
+            def _():
+                residual(td, weight)
+
+            @pl.when(in_d & jnp.logical_not(ending))
+            def _():
+                residual_out(td)
+
+            @pl.when(ending)
+            def _():
+                residual_final(td)
+
+            @pl.when(in_c)
+            def _():
+                products(tc, 0)
+
+            @pl.when(in_c)
+            def _():
+                gather_third(tc, step_net)
+
+            @pl.when(in_b)
+            def _():
+                take_step(tb)
+                gather_open(tb, step_net)
+
+            @pl.when(in_b & wrap_up)
+            def _():
+                coef_open(tb)
+
+            @pl.when((i > 2 + rounds - STREAMS + 1) & in_c)
+            def _():
+                gather_second(tc, coef_net)
+
+            @pl.when(i > 2 + rounds - STREAMS + 2)
+            def _():
+                gather_third(td, coef_net)
+
+            @pl.when(in_c)
+            def _():
+                products(tc, -1)
+                products(tc, 1)
+
             return carry
 
-        lax.fori_loop(0, SWEEPS, sweep, 0)
-
-        def coef_out(t):
-            for h in range(2):
-                for pm in range(2):
-                    wg[t, zpos, ypos, h, :, pl.ds(pm * LANES, LANES)] = wown[t, h, pm]
-            yield from gather(t, wg, w_send, w_recv)
-
-        def rmsg(t, k):
-            return xmsg(t, k, rfin.at[t, feat], rfin.at[t, feat], rf_recv)
-
-        def last(t):
-            yield from feat_phase(t, STEP_WEIGHT, final=True)
-            rfin[t, feat] = rown[t]
-            for k in range(1, FEATS):
-                rmsg(t, k).start()
-            yield
-            for k in range(1, FEATS):
-                rmsg(t, k).wait()
-
-        rfin[0, feat] = rown[0]
-        for k in range(1, FEATS):
-            rmsg(0, k).start()
-        weave(ORDER_END, last(1), coef_out(0), coef_out(1))
-        for k in range(1, FEATS):
-            rmsg(0, k).wait()
+        lax.fori_loop(0, rounds + STREAMS + 1, one_pass, 0)
+
+        for t in range(STREAMS):
+            gather_close(t, coef_net)
+            for k in range(1, FEATS):
+                fmsg(t, k).wait()
 
         for q in range(4):
             def flop(c, carry, q=q):

time: 275 us -> 235 us (0.85)
  Pallas kernels: 269 us -> 229 us
    pallas_call x1, Pallas kernels: 269 us -> 229 us  [local(): pl.pallas_call(make_kernel(rows * samp_size, tgt), out_shape=(jax.ShapeDt...]
where the time goes in v3:
time: 235 us; the launch traced here: 234 us
  Pallas kernels  229 us (97%)
  local copies, waits for them, and re-layouts  5.22 us (2%)
    pallas_call x1, Pallas kernels, local(): pl.pallas_call(make_kernel(rows * samp_size, tgt), out_shape=(jax.ShapeDt...  229 us
    unnamed x4, local copies, waits for them, and re-layouts  5.22 us

profile of v3, /device:TPU:1, one launch (start us, length us, event | category | flops | bytes accessed | tf_op | source)
XLA Modules:
  0.0 234.4 jit_solution(17927984077255394526)
XLA Ops:
  0.6 228.6 %shard_map.68 = (f32[32,256,128]{2,1,0:T(8,128)}, f32[4,128,128]{2,1,0:T(8,128)}) custom-call(bf16[512,8192]{1,0:T(8,128)(2,1)} %x_hbm.1, f32[512,128]{1,0:T(8,128)} %y_hbm.1, f32[32,256,128]{2,1,0:T(8,128)} %bitcast.5, f32[64,128]{1,0:T(8,128)} %bitcast.8, f32[1,128]{1,0:T(1,128)} %bitcast.9), custom_call_target="tpu_custom_call" | custom-call | tf_op jit(solution)/shard_map/pallas_call | solution.py:418
  229.2 0.0 copy-start
  229.2 4.5 %copy.9 = f32[8192,128]{1,0:T(8,128)} copy(f32[8192,128]{1,0:T(8,128)} %bitcast.6) | data formatting | bytes 8388608
  233.7 0.0 copy-done
  233.7 0.7 copy.10
Async XLA Ops:
  229.2 4.5 %copy-start = (f32[4,128,128]{2,1,0:T(8,128)S(1)}, f32[4,128,128]{2,1,0:T(8,128)}, u32[]{:S(2)}) copy-start(f32[4,128,128]{2,1,0:T(8,128)} %get-tuple-element.5) | copy-start | bytes 786436

commit v4 on v3

--- a/solution.py
+++ b/solution.py
@@ -19,12 +19,26 @@
 BF16 = jnp.bfloat16
 
 
+def flip_results(w_ref, r_ref, coef_ref, resid_ref):
+    for y in range(2):
+        for h in range(2):
+            for pm in range(2):
+                cols = [w_ref[t, 0, y, h, :, pl.ds(pm * LANES, LANES)] for t in range(STREAMS)]
+                coef_ref[pl.ds(((y * 2 + h) * 2 + pm) * LANES, LANES), :] = jnp.concatenate(cols, axis=0).T
+
+    @pl.when(pl.program_id(0) == 0)
+    def _():
+        for xq in range(4):
+            cols = [r_ref[t, 2 * xq + side] for t in range(STREAMS) for side in range(2)]
+            resid_ref[pl.ds(xq * LANES, LANES), :] = jnp.concatenate(cols, axis=0).T
+
+
 def make_kernel(total_rows, tgt):
     half = tgt // 2
     inv_rows = 1.0 / total_rows
 
     def kernel(x_hbm, y_hbm, w0_hbm, eta_ref, lam_ref, w_out, r_out,
-               xv, wst, yst, rnat, flat, sg, wg, gt, fin, din, cin, r2in, wown, lamb, rt, acc,
+               xv, xt, wst, yst, uacc, sg, wg, gt, fin, din, cin, r2in, wown, lamb, rt, acc,
                ub, urecv, rbuf, rown, rfin,
                xsem, wsem, ysem, rs_send, rs_recv, ag_recv, w_send, w_recv, x_send, u_recv, r_recv, rf_recv):
         samp = lax.axis_index("samp")
@@ -52,12 +66,13 @@
             return lax.rem(feat + k, FEATS)
 
         x_copies = [pltpu.make_async_copy(x_hbm.at[:, pl.ds(c * 256, 256)], xv.at[c], xsem.at[c]) for c in range(32)]
-        w_copy = pltpu.make_async_copy(w0_hbm.at[pl.ds(samp * 2, 2)], wst.at[pl.ds(0, 2)], wsem.at[0])
+        w_copies = [pltpu.make_async_copy(w0_hbm.at[pl.ds(8 * q, 8)], wst.at[pl.ds(8 * q, 8)], wsem.at[q]) for q in range(4)]
         y_copy = pltpu.make_async_copy(y_hbm.at[pl.ds(pl.multiple_of((feat // 2) * LANES, LANES), LANES)], yst, ysem)
-        w_copy.start()
         y_copy.start()
-        for copy in x_copies:
-            copy.start()
+        for q in range(4):
+            w_copies[q].start()
+            for c in range(8 * q, 8 * q + 8):
+                x_copies[c].start()
 
         barrier = pltpu.get_barrier_semaphore()
         for nbr in (z_plus, z_minus, y_plus, y_minus, dev(wrap(zpos + 2), ypos), dev(zpos, wrap(ypos + 2))):
@@ -144,18 +159,22 @@
                 for idx in range(AG_MSGS):
                     ag(t, h, idx, *net).wait_send()
 
-        def slopes(t, io):
-            for h in range(2):
-                for js in range(RING):
-                    zi, yi = place(h, io, ORDER[js])
-                    res = jnp.dot(rt[t], xv[(zi * RING + yi) * 2 + h], preferred_element_type=F32)
-                    gt[t, h, io, 0, js] = res[:, :LANES]
-                    gt[t, h, io, 1, js] = res[:, LANES:]
-                    if io == 2 and js % 2:
-                        rs1(t, h, "F", 0, js // 2).start()
-                        rs1(t, h, "F", 1, js // 2).start()
-                if io % 2:
-                    rs1(t, h, "D", io // 2, 0).start()
+        def slopes(t, *ios):
+            for io in ios:
+                for h in range(2):
+                    for js in range(RING):
+                        zi, yi = place(h, io, ORDER[js])
+                        res = jnp.dot(rt[t], xv[(zi * RING + yi) * 2 + h], preferred_element_type=F32)
+                        gt[t, h, io, 0, js] = res[:, :LANES]
+                        gt[t, h, io, 1, js] = res[:, LANES:]
+            for io in ios:
+                for h in range(2):
+                    if io == 2:
+                        for part in range(2):
+                            rs1(t, h, "F", 0, part).start()
+                            rs1(t, h, "F", 1, part).start()
+                    elif io:
+                        rs1(t, h, "D", io // 2, 0).start()
 
         def sum_first(t):
             for part in range(2):
@@ -210,7 +229,7 @@
                 for o2 in (0, -1, 1, 2):
                     zi, yi = place(h, o1, o2)
                     c = (zi * RING + yi) * 2 + h
-                    prod = lax.dot_general(sg[t, zi, yi, h], xv[c], (((1,), (1,)), ((), ())), preferred_element_type=F32)
+                    prod = jnp.dot(sg[t, zi, yi, h], xt[c], preferred_element_type=F32)
                     part = prod if part is None else part + prod
             acc[t] = part if o1 == 0 else acc[t] + part
 
@@ -229,6 +248,9 @@
         def blocks_out(t):
             for j in range(FEATS):
                 ub[t, j] = acc[t, pl.ds((j % 2) * half, half), pl.ds((j // 2) * LANES, LANES)].astype(BF16)
+            blocks_send(t)
+
+        def blocks_send(t):
             for k in range(1, FEATS):
                 umsg(t, k).start()
             urecv[t, feat] = ub[t, feat]
@@ -266,19 +288,46 @@
         yst[...] = y_cols
         for t in range(STREAMS):
             rown[t] = yst[pl.ds(pl.multiple_of(t * tgt + core * half, half), half), :]
-        w_copy.wait()
+        for q in range(4):
+            w_copies[q].wait()
+            for c in range(8 * q, 8 * q + 8):
+                x_copies[c].wait()
+
+            def start_block(g, carry, q=q):
+                part = None
+                for j in range(4):
+                    c = 8 * q + 4 * g + j
+                    prod = jnp.dot(xv[c], wst[c].astype(BF16), preferred_element_type=F32)
+                    part = prod if part is None else part + prod
+                uacc[...] = uacc[...] + part
+                return carry
+
+            if q == 0:
+                uacc[...] = jnp.zeros_like(uacc)
+            lax.fori_loop(0, 2, start_block, 0)
+        for xq in range(4):
+            cols = uacc[pl.ds(xq * LANES, LANES), :].T
+            for t in range(STREAMS):
+                for side in range(2):
+                    row = t * tgt + side * half
+                    ub[t, 2 * xq + side] = cols[row:row + half].astype(BF16)
+        for t in range(STREAMS):
+            blocks_send(t)
         for h in range(2):
             for pm in range(2):
-                cols = wst[h, pl.ds(pm * LANES, LANES), :].T
+                cols = wst[samp * 2 + h, pl.ds(pm * LANES, LANES), :].T
                 for t in range(STREAMS):
-                    mine = cols[t * tgt:(t + 1) * tgt]
-                    wown[t, h, pm] = mine
-                    sg[t, zpos, ypos, h, :, pl.ds(pm * LANES, LANES)] = mine.astype(BF16)
-
-        for t in range(STREAMS):
-            gather_open(t, step_net)
-        for copy in x_copies:
-            copy.wait()
+                    wown[t, h, pm] = cols[t * tgt:(t + 1) * tgt]
+
+        def turn(c, carry):
+            xt[c] = xv[c].T
+            return carry
+
+        lax.fori_loop(0, 20, turn, 0)
+        for t in range(STREAMS):
+            residual(t, 1.0)
+            residual_out(t)
+        lax.fori_loop(20, 32, turn, 0)
 
         rounds = STREAMS * SWEEPS
 
@@ -286,11 +335,10 @@
             ta, tb, tc, td = (lax.rem(i + off, STREAMS) for off in (2, 1, 0, 3))
             in_a = (i >= 2) & (i < 2 + rounds)
             in_b = (i >= 3) & (i < 3 + rounds)
-            in_c = i < STREAMS + rounds
-            in_d = i >= 1
+            in_c = (i >= STREAMS) & (i < STREAMS + rounds)
+            in_d = i >= 1 + STREAMS
             wrap_up = i >= 3 + rounds - STREAMS
             ending = i >= 1 + rounds
-            weight = jnp.where(i <= STREAMS, 1.0, STEP_WEIGHT).astype(F32)
 
             @pl.when(in_a)
             def _():
@@ -311,11 +359,17 @@
             def _():
                 gather_second(tc, step_net)
 
+            @pl.when(i > 2 + rounds - STREAMS + 2)
+            def _():
+                gather_third(td, coef_net)
+
+            @pl.when((i > 2 + rounds - STREAMS + 1) & in_c)
+            def _():
+                gather_second(tc, coef_net)
+
             @pl.when(in_a)
             def _():
-                slopes(ta, 1)
-                slopes(ta, 3)
-                slopes(ta, 0)
+                slopes(ta, 1, 3, 0)
 
             @pl.when(in_a)
             def _():
@@ -323,7 +377,7 @@
 
             @pl.when(in_d)
             def _():
-                residual(td, weight)
+                residual(td, STEP_WEIGHT)
 
             @pl.when(in_d & jnp.logical_not(ending))
             def _():
@@ -350,14 +404,6 @@
             def _():
                 coef_open(tb)
 
-            @pl.when((i > 2 + rounds - STREAMS + 1) & in_c)
-            def _():
-                gather_second(tc, coef_net)
-
-            @pl.when(i > 2 + rounds - STREAMS + 2)
-            def _():
-                gather_third(td, coef_net)
-
             @pl.when(in_c)
             def _():
                 products(tc, -1)
@@ -365,33 +411,19 @@
 
             return carry
 
-        lax.fori_loop(0, rounds + STREAMS + 1, one_pass, 0)
-
-        for t in range(STREAMS):
-            gather_close(t, coef_net)
+        lax.fori_loop(2, rounds + STREAMS + 1, one_pass, 0)
+
+        w_done = [pltpu.make_async_copy(wg.at[t], w_out.at[t], wsem.at[t]) for t in range(STREAMS)]
+        for t in range(STREAMS):
             for k in range(1, FEATS):
                 fmsg(t, k).wait()
-
-        for q in range(4):
-            def flop(c, carry, q=q):
-                for pm in range(2):
-                    for t in range(STREAMS):
-                        flat[pm, t * tgt:(t + 1) * tgt] = wg[t, q, c // 2, lax.rem(c, 2), :, pl.ds(pm * LANES, LANES)]
-                for pm in range(2):
-                    wst[8 * q + c, pl.ds(pm * LANES, LANES), :] = flat[pm].T
-                return carry
-
-            lax.fori_loop(0, 8, flop, 0)
-            pltpu.make_async_copy(wst.at[pl.ds(8 * q, 8)], w_out.at[pl.ds(8 * q, 8)], wsem.at[q]).start()
-        for xc in range(4):
-            for t in range(STREAMS):
-                for core_id in range(2):
-                    flat[xc % 2, pl.ds(t * tgt + core_id * half, half), :] = rfin[t, 2 * xc + core_id]
-            rnat[xc] = flat[xc % 2].T
-        r_done = pltpu.make_async_copy(rnat, r_out, ysem)
+        r_done = pltpu.make_async_copy(rfin, r_out, ysem)
         r_done.start()
-        for q in range(4):
-            pltpu.make_async_copy(wst.at[pl.ds(8 * q, 8)], w_out.at[pl.ds(8 * q, 8)], wsem.at[q]).wait()
+        for t in range(STREAMS):
+            gather_close(t, coef_net)
+            w_done[t].start()
+        for t in range(STREAMS):
+            w_done[t].wait()
         r_done.wait()
 
     return kernel
@@ -417,15 +449,15 @@
         vmem_spec = pl.BlockSpec(memory_space=pltpu.VMEM)
         w_t, r_t = pl.pallas_call(
             make_kernel(rows * samp_size, tgt),
-            out_shape=(jax.ShapeDtypeStruct((32, 256, n_tgt), F32), jax.ShapeDtypeStruct((rows // LANES, LANES, n_tgt), F32)),
+            out_shape=(jax.ShapeDtypeStruct(own, F32), jax.ShapeDtypeStruct((STREAMS, FEATS, half, LANES), F32)),
             in_specs=[any_spec, any_spec, any_spec, vmem_spec, vmem_spec],
             out_specs=(any_spec, any_spec),
             scratch_shapes=[
                 vm((32, rows, 256), BF16),
+                vm((32, 256, rows), BF16),
                 vm((32, 256, LANES), F32),
                 vm((LANES, LANES), F32),
-                vm((rows // LANES, LANES, n_tgt), F32),
-                vm((2, LANES, n_tgt), F32),
+                vm((rows, n_tgt), F32),
                 vm(own, BF16),
                 vm(own, F32),
                 vm((STREAMS, 2, RING, 2, RING, tgt, LANES), F32),
@@ -457,8 +489,16 @@
             ],
             compiler_params=pltpu.CompilerParams(collective_id=0, has_side_effects=True, vmem_limit_bytes=60 * 1024 * 1024),
         )(design, targets, coef_init.reshape(32, 256, n_tgt), step_sizes.reshape(cols // LANES, LANES), ridge_weights.reshape(1, n_tgt))
-        coef = w_t.reshape(cols, n_tgt)
-        resid = r_t.reshape(rows, n_tgt)
+        coef, resid = pl.pallas_call(
+            flip_results,
+            grid=(8,),
+            in_specs=[
+                pl.BlockSpec((STREAMS, 1, 2, 2, tgt, 256), lambda g: (0, g // 2, g % 2, 0, 0, 0)),
+                pl.BlockSpec((STREAMS, FEATS, half, LANES), lambda g: (0, 0, 0, 0)),
+            ],
+            out_specs=(pl.BlockSpec((cols // 8, n_tgt), lambda g: (g, 0)), pl.BlockSpec((rows, n_tgt), lambda g: (0, 0))),
+            out_shape=(jax.ShapeDtypeStruct((cols, n_tgt), F32), jax.ShapeDtypeStruct((rows, n_tgt), F32)),
+        )(w_t, r_t)
         return coef, resid
 
     return jax.shard_map(local, mesh=mesh, in_specs=(design_spec, rows_spec, coef_spec, step_spec, ridge_spec), out_specs=(coef_spec, rows_spec), check_vma=False)

time: 235 us -> 221 us (0.940)
  Pallas kernels: 229 us -> 220 us
  local copies, waits for them, and re-layouts: 5.22 us -> 0 us
    pallas_call x1, Pallas kernels: 229 us -> 212 us  [local(): pl.pallas_call(make_kernel(rows * samp_size, tgt), out_shape=(jax.ShapeDt...]
    pallas_call x0 -> x1, Pallas kernels: none -> 7.5 us  [local(): pl.pallas_call(flip_results, grid=(8,), in_specs=[pl.BlockSpec((STREAMS,...]
    unnamed x4 -> x0, local copies, waits for them, and re-layouts: 5.22 us -> none
where the time goes in v4:
time: 221 us
  Pallas kernels  220 us (100%)
    pallas_call x1, Pallas kernels, local(): pl.pallas_call(make_kernel(rows * samp_size, tgt), out_shape=(jax.ShapeDt...  212 us
    pallas_call x1, Pallas kernels, local(): pl.pallas_call(flip_results, grid=(8,), in_specs=[pl.BlockSpec((STREAMS,...  7.5 us

profile of v4, /device:TPU:1, one launch (start us, length us, event | category | flops | bytes accessed | tf_op | source)
XLA Modules:
  0.0 220.6 jit_solution(16115876444333298834)
XLA Ops:
  0.6 212.4 %shard_map.68 = (f32[4,4,4,2,32,256]{5,4,3,2,1,0:T(8,128)}, f32[4,8,16,128]{3,2,1,0:T(8,128)}) custom-call(bf16[512,8192]{1,0:T(8,128)(2,1)} %x_hbm.1, f32[512,128]{1,0:T(8,128)} %y_hbm.1, f32[32,256,128]{2,1,0:T(8,128)} %bitcast.3, f32[64,128]{1,0:T(8,128)} %bitcast.4, f32[1,128]{1,0:T(1,128)} %bitcast.5), custom_call_target="tpu_custom_call" | custom-call | tf_op jit(solution)/shard_map/pallas_call | solution.py:450
  213.1 7.5 %shard_map.69 = (f32[8192,128]{1,0:T(8,128)}, f32[512,128]{1,0:T(8,128)}) custom-call(f32[4,4,4,2,32,256]{5,4,3,2,1,0:T(8,128)} %get-tuple-element.4.w_ref, f32[4,8,16,128]{3,2,1,0:T(8,128)} %get-tuple-element.5.r_ref), custom_call_target="tpu_custom_call" | custom-call | tf_op jit(solution)/shard_map/pallas_call | solution.py:492

commit v5 on v4

--- a/solution.py
+++ b/solution.py
@@ -19,28 +19,39 @@
 BF16 = jnp.bfloat16
 
 
-def flip_results(w_ref, r_ref, coef_ref, resid_ref):
-    for y in range(2):
-        for h in range(2):
-            for pm in range(2):
-                cols = [w_ref[t, 0, y, h, :, pl.ds(pm * LANES, LANES)] for t in range(STREAMS)]
-                coef_ref[pl.ds(((y * 2 + h) * 2 + pm) * LANES, LANES), :] = jnp.concatenate(cols, axis=0).T
-
-    @pl.when(pl.program_id(0) == 0)
-    def _():
-        for xq in range(4):
-            cols = [r_ref[t, 2 * xq + side] for t in range(STREAMS) for side in range(2)]
-            resid_ref[pl.ds(xq * LANES, LANES), :] = jnp.concatenate(cols, axis=0).T
+def flip_results(w_hbm, r_hbm, coef_hbm, resid_hbm, w_in, r_in, coef, resid, in_sem, out_sem, r_sem):
+    loads = [pltpu.make_async_copy(w_hbm.at[:, p // 2, pl.ds(p % 2 * 2, 2)], w_in.at[p], in_sem.at[p]) for p in range(8)]
+    stores = [pltpu.make_async_copy(coef.at[p], coef_hbm.at[pl.ds(p * 1024, 1024)], out_sem.at[p]) for p in range(8)]
+    r_load = pltpu.make_async_copy(r_hbm, r_in, r_sem.at[0])
+    r_store = pltpu.make_async_copy(resid, resid_hbm, r_sem.at[1])
+    r_load.start()
+    for load in loads:
+        load.start()
+    r_load.wait()
+    for xq in range(4):
+        cols = [r_in[t, :, pl.ds(xq * LANES, LANES)] for t in range(STREAMS)]
+        resid[pl.ds(xq * LANES, LANES), :] = jnp.concatenate(cols, axis=0).T
+    r_store.start()
+    for p in range(8):
+        loads[p].wait()
+        for y in range(2):
+            for h in range(2):
+                cols = [w_in[p, t, y, h] for t in range(STREAMS)]
+                coef[p, pl.ds((y * 2 + h) * 256, 256), :] = jnp.concatenate(cols, axis=0).T
+        stores[p].start()
+    for p in range(8):
+        stores[p].wait()
+    r_store.wait()
 
 
 def make_kernel(total_rows, tgt):
     half = tgt // 2
     inv_rows = 1.0 / total_rows
 
-    def kernel(x_hbm, y_hbm, w0_hbm, eta_ref, lam_ref, w_out, r_out,
-               xv, xt, wst, yst, uacc, sg, wg, gt, fin, din, cin, r2in, wown, lamb, rt, acc,
-               ub, urecv, rbuf, rown, rfin,
-               xsem, wsem, ysem, rs_send, rs_recv, ag_recv, w_send, w_recv, x_send, u_recv, r_recv, rf_recv):
+    def kernel(x_hbm, y_hbm, w0_hbm, eta_hbm, lam_hbm, w_out, r_out,
+               eta_ref, lam_ref, xv, xt, wst, yst, uacc, sg, wg, gt, fin, din, cin, r2in, wown, lamb, rt, acc,
+               ub, urecv, rown,
+               xsem, wsem, psem, ysem, rs_send, rs_recv, ag_recv, w_send, w_recv, x_send, u_recv):
         samp = lax.axis_index("samp")
         feat = lax.axis_index("feat")
         zpos = samp // RING
@@ -67,19 +78,23 @@
 
         x_copies = [pltpu.make_async_copy(x_hbm.at[:, pl.ds(c * 256, 256)], xv.at[c], xsem.at[c]) for c in range(32)]
         w_copies = [pltpu.make_async_copy(w0_hbm.at[pl.ds(8 * q, 8)], wst.at[pl.ds(8 * q, 8)], wsem.at[q]) for q in range(4)]
-        y_copy = pltpu.make_async_copy(y_hbm.at[pl.ds(pl.multiple_of((feat // 2) * LANES, LANES), LANES)], yst, ysem)
-        y_copy.start()
+        y_copy = pltpu.make_async_copy(y_hbm, yst, ysem)
+        eta_copy = pltpu.make_async_copy(eta_hbm, eta_ref, psem.at[0])
+        lam_copy = pltpu.make_async_copy(lam_hbm, lam_ref, psem.at[1])
         for q in range(4):
             w_copies[q].start()
             for c in range(8 * q, 8 * q + 8):
                 x_copies[c].start()
+
+        y_copy.start()
+        eta_copy.start()
+        lam_copy.start()
 
         barrier = pltpu.get_barrier_semaphore()
         for nbr in (z_plus, z_minus, y_plus, y_minus, dev(wrap(zpos + 2), ypos), dev(zpos, wrap(ypos + 2))):
             pl.semaphore_signal(barrier, inc=1, device_id=nbr, device_id_type=MESH_ID)
         for k in range(1, FEATS):
             pl.semaphore_signal(barrier, inc=1, device_id=(0, samp, peer(k)), device_id_type=MESH_ID)
-        pl.semaphore_wait(barrier, 6 + FEATS - 1)
 
         def remote(src, dst, send, recv, to):
             return pltpu.make_async_remote_copy(src_ref=src, dst_ref=dst, send_sem=send, recv_sem=recv, device_id=to, device_id_type=MESH_ID)
@@ -233,61 +248,28 @@
                     part = prod if part is None else part + prod
             acc[t] = part if o1 == 0 else acc[t] + part
 
-        def xmsg(t, k, src, dst, recv):
-            return remote(src, dst, x_send.at[t, k], recv.at[t, k], (0, samp, peer(k)))
-
-        def umsg(t, k):
-            return xmsg(t, k, ub.at[t, peer(k)], urecv.at[t, feat], u_recv)
-
-        def rmsg(t, k):
-            return xmsg(t, k, rbuf.at[t, feat], rbuf.at[t, feat], r_recv)
-
-        def fmsg(t, k):
-            return xmsg(t, k, rfin.at[t, feat], rfin.at[t, feat], rf_recv)
-
-        def blocks_out(t):
-            for j in range(FEATS):
-                ub[t, j] = acc[t, pl.ds((j % 2) * half, half), pl.ds((j // 2) * LANES, LANES)].astype(BF16)
-            blocks_send(t)
-
-        def blocks_send(t):
+        def umsg(t, k, side):
+            return remote(ub.at[t], urecv.at[side, t, feat], x_send.at[t, k], u_recv.at[side, t, k], (0, samp, peer(k)))
+
+        def blocks_send(t, side):
             for k in range(1, FEATS):
-                umsg(t, k).start()
-            urecv[t, feat] = ub[t, feat]
-
-        def residual(t, weight):
+                umsg(t, k, side).start()
+            urecv[side, t, feat] = ub[t]
+
+        def blocks_out(t, side):
+            ub[t] = acc[t].astype(BF16)
+            blocks_send(t, side)
+
+        def residual(t, side, weight):
             for k in range(1, FEATS):
-                umsg(t, k).wait()
-            total = urecv[t, 0].astype(F32)
+                umsg(t, k, side).wait()
+            total = urecv[side, t, 0].astype(F32)
             for j in range(1, FEATS):
-                total = total + urecv[t, j].astype(F32)
-            rown[t] = rown[t] - weight * total
-
-        def residual_out(t):
-            rbuf[t, feat] = rown[t].astype(BF16)
-            for k in range(1, FEATS):
-                rmsg(t, k).start()
-
-        def residual_final(t):
-            rfin[t, feat] = rown[t]
-            for k in range(1, FEATS):
-                fmsg(t, k).start()
-
-        def residual_in(t):
-            for k in range(1, FEATS):
-                rmsg(t, k).wait()
-            for j in range(FEATS):
-                rt[t, pl.ds((j % 2) * half, half), pl.ds((j // 2) * LANES, LANES)] = rbuf[t, j]
-
-        lam_cols = jnp.broadcast_to(lam_ref[...], (LANES, LANES)).T
-        for t in range(STREAMS):
-            lamb[t] = lam_cols[t * tgt:(t + 1) * tgt]
-        y_copy.wait()
-        y_cols = yst[...].T
-        core = lax.rem(feat, 2)
-        yst[...] = y_cols
-        for t in range(STREAMS):
-            rown[t] = yst[pl.ds(pl.multiple_of(t * tgt + core * half, half), half), :]
+                total = total + urecv[side, t, j].astype(F32)
+            resid = rown[t] - weight * total
+            rown[t] = resid
+            rt[t] = resid.astype(BF16)
+
         for q in range(4):
             w_copies[q].wait()
             for c in range(8 * q, 8 * q + 8):
@@ -308,11 +290,20 @@
         for xq in range(4):
             cols = uacc[pl.ds(xq * LANES, LANES), :].T
             for t in range(STREAMS):
-                for side in range(2):
-                    row = t * tgt + side * half
-                    ub[t, 2 * xq + side] = cols[row:row + half].astype(BF16)
+                ub[t, :, pl.ds(xq * LANES, LANES)] = cols[t * tgt:(t + 1) * tgt].astype(BF16)
+        pl.semaphore_wait(barrier, 6 + FEATS - 1)
         for t in range(STREAMS):
-            blocks_send(t)
+            blocks_send(t, 0)
+        eta_copy.wait()
+        lam_copy.wait()
+        lam_cols = jnp.broadcast_to(lam_ref[...], (LANES, LANES)).T
+        for t in range(STREAMS):
+            lamb[t] = lam_cols[t * tgt:(t + 1) * tgt]
+        y_copy.wait()
+        for xq in range(4):
+            cols = yst[pl.ds(xq * LANES, LANES), :].T
+            for t in range(STREAMS):
+                rown[t, :, pl.ds(xq * LANES, LANES)] = cols[t * tgt:(t + 1) * tgt]
         for h in range(2):
             for pm in range(2):
                 cols = wst[samp * 2 + h, pl.ds(pm * LANES, LANES), :].T
@@ -323,11 +314,8 @@
             xt[c] = xv[c].T
             return carry
 
-        lax.fori_loop(0, 20, turn, 0)
-        for t in range(STREAMS):
-            residual(t, 1.0)
-            residual_out(t)
-        lax.fori_loop(20, 32, turn, 0)
+        lax.fori_loop(0, 32, turn, 0)
+        residual(0, 0, 1.0)
 
         rounds = STREAMS * SWEEPS
 
@@ -338,11 +326,11 @@
             in_c = (i >= STREAMS) & (i < STREAMS + rounds)
             in_d = i >= 1 + STREAMS
             wrap_up = i >= 3 + rounds - STREAMS
-            ending = i >= 1 + rounds
+            side = lax.rem((i - 1) // STREAMS, 2)
+            weight = jnp.where(i <= STREAMS, 1.0, STEP_WEIGHT).astype(F32)
 
             @pl.when(in_a)
             def _():
-                residual_in(ta)
                 slopes(ta, 2)
 
             @pl.when(in_b)
@@ -353,7 +341,7 @@
             def _():
                 gather_close(td, step_net)
                 products(td, 2)
-                blocks_out(td)
+                blocks_out(td, side)
 
             @pl.when(in_c)
             def _():
@@ -374,18 +362,6 @@
             @pl.when(in_a)
             def _():
                 sum_first(ta)
-
-            @pl.when(in_d)
-            def _():
-                residual(td, STEP_WEIGHT)
-
-            @pl.when(in_d & jnp.logical_not(ending))
-            def _():
-                residual_out(td)
-
-            @pl.when(ending)
-            def _():
-                residual_final(td)
 
             @pl.when(in_c)
             def _():
@@ -409,16 +385,14 @@
                 products(tc, -1)
                 products(tc, 1)
 
+            residual(td, side, weight)
             return carry
 
         lax.fori_loop(2, rounds + STREAMS + 1, one_pass, 0)
 
+        r_done = pltpu.make_async_copy(rown, r_out, ysem)
+        r_done.start()
         w_done = [pltpu.make_async_copy(wg.at[t], w_out.at[t], wsem.at[t]) for t in range(STREAMS)]
-        for t in range(STREAMS):
-            for k in range(1, FEATS):
-                fmsg(t, k).wait()
-        r_done = pltpu.make_async_copy(rfin, r_out, ysem)
-        r_done.start()
         for t in range(STREAMS):
             gather_close(t, coef_net)
             w_done[t].start()
@@ -446,17 +420,18 @@
         vm = pltpu.VMEM
         dma = pltpu.SemaphoreType.DMA
         any_spec = pl.BlockSpec(memory_space=pl.ANY)
-        vmem_spec = pl.BlockSpec(memory_space=pltpu.VMEM)
         w_t, r_t = pl.pallas_call(
             make_kernel(rows * samp_size, tgt),
-            out_shape=(jax.ShapeDtypeStruct(own, F32), jax.ShapeDtypeStruct((STREAMS, FEATS, half, LANES), F32)),
-            in_specs=[any_spec, any_spec, any_spec, vmem_spec, vmem_spec],
+            out_shape=(jax.ShapeDtypeStruct(own, F32), jax.ShapeDtypeStruct((STREAMS, tgt, rows), F32)),
+            in_specs=[any_spec] * 5,
             out_specs=(any_spec, any_spec),
             scratch_shapes=[
+                vm((cols // LANES, LANES), F32),
+                vm((1, n_tgt), F32),
                 vm((32, rows, 256), BF16),
                 vm((32, 256, rows), BF16),
                 vm((32, 256, LANES), F32),
-                vm((LANES, LANES), F32),
+                vm((rows, LANES), F32),
                 vm((rows, n_tgt), F32),
                 vm(own, BF16),
                 vm(own, F32),
@@ -469,13 +444,12 @@
                 vm((STREAMS, tgt, LANES), F32),
                 vm((STREAMS, tgt, rows), BF16),
                 vm((STREAMS, tgt, rows), F32),
-                vm((STREAMS, FEATS, half, LANES), BF16),
-                vm((STREAMS, FEATS, half, LANES), BF16),
-                vm((STREAMS, FEATS, half, LANES), BF16),
-                vm((STREAMS, half, LANES), F32),
-                vm((STREAMS, FEATS, half, LANES), F32),
+                vm((STREAMS, tgt, rows), BF16),
+                vm((2, STREAMS, FEATS, tgt, rows), BF16),
+                vm((STREAMS, tgt, rows), F32),
                 dma((32,)),
                 dma((4,)),
+                dma((2,)),
                 dma,
                 dma((STREAMS, 2 * AG_MSGS)),
                 dma((STREAMS, RS_MSGS)),
@@ -483,21 +457,24 @@
                 dma((STREAMS, 2 * AG_MSGS)),
                 dma((STREAMS, 2 * AG_MSGS)),
                 dma((STREAMS, FEATS)),
-                dma((STREAMS, FEATS)),
-                dma((STREAMS, FEATS)),
-                dma((STREAMS, FEATS)),
+                dma((2, STREAMS, FEATS)),
             ],
             compiler_params=pltpu.CompilerParams(collective_id=0, has_side_effects=True, vmem_limit_bytes=60 * 1024 * 1024),
         )(design, targets, coef_init.reshape(32, 256, n_tgt), step_sizes.reshape(cols // LANES, LANES), ridge_weights.reshape(1, n_tgt))
         coef, resid = pl.pallas_call(
             flip_results,
-            grid=(8,),
-            in_specs=[
-                pl.BlockSpec((STREAMS, 1, 2, 2, tgt, 256), lambda g: (0, g // 2, g % 2, 0, 0, 0)),
-                pl.BlockSpec((STREAMS, FEATS, half, LANES), lambda g: (0, 0, 0, 0)),
+            in_specs=[any_spec, any_spec],
+            out_specs=(any_spec, any_spec),
+            out_shape=(jax.ShapeDtypeStruct((cols, n_tgt), F32), jax.ShapeDtypeStruct((rows, n_tgt), F32)),
+            scratch_shapes=[
+                vm((8, STREAMS, 2, 2, tgt, 256), F32),
+                vm((STREAMS, tgt, rows), F32),
+                vm((8, cols // 8, n_tgt), F32),
+                vm((rows, n_tgt), F32),
+                dma((8,)),
+                dma((8,)),
+                dma((2,)),
             ],
-            out_specs=(pl.BlockSpec((cols // 8, n_tgt), lambda g: (g, 0)), pl.BlockSpec((rows, n_tgt), lambda g: (0, 0))),
-            out_shape=(jax.ShapeDtypeStruct((cols, n_tgt), F32), jax.ShapeDtypeStruct((rows, n_tgt), F32)),
         )(w_t, r_t)
         return coef, resid
 

time: 221 us -> 205 us (0.928)
  Pallas kernels: 220 us -> 204 us
    pallas_call x1, Pallas kernels: 212 us -> 199 us  [local(): pl.pallas_call(make_kernel(rows * samp_size, tgt), out_shape=(jax.ShapeDt...]
    pallas_call x1, Pallas kernels: 7.5 us -> 4.77 us  [local(): pl.pallas_call(flip_results, in_specs=[any_spec, any_spec], out_specs=(an...]
where the time goes in v5:
time: 205 us; the launch traced here: 204 us
  Pallas kernels  204 us (100%)
    pallas_call x1, Pallas kernels, local(): pl.pallas_call(make_kernel(rows * samp_size, tgt), out_shape=(jax.ShapeDt...  199 us
    pallas_call x1, Pallas kernels, local(): pl.pallas_call(flip_results, in_specs=[any_spec, any_spec], out_specs=(an...  4.77 us

profile of v5, /device:TPU:1, one launch (start us, length us, event | category | flops | bytes accessed | tf_op | source)
XLA Modules:
  0.0 204.4 jit_solution(4678720223093304726)
XLA Ops:
  0.6 199.0 %shard_map.68 = (f32[4,4,4,2,32,256]{5,4,3,2,1,0:T(8,128)}, f32[4,32,512]{2,1,0:T(8,128)}) custom-call(bf16[512,8192]{1,0:T(8,128)(2,1)} %x_hbm.1, f32[512,128]{1,0:T(8,128)} %y_hbm.1, f32[32,256,128]{2,1,0:T(8,128)} %bitcast.3, f32[64,128]{1,0:T(8,128)} %bitcast.4, f32[1,128]{1,0:T(1,128)} %bitcast.5), custom_call_target="tpu_custom_call" | custom-call | tf_op jit(solution)/shard_map/pallas_call | solution.py:423
  199.7 4.8 %shard_map.69 = (f32[8192,128]{1,0:T(8,128)}, f32[512,128]{1,0:T(8,128)}) custom-call(f32[4,4,4,2,32,256]{5,4,3,2,1,0:T(8,128)} %get-tuple-element.4.w_hbm, f32[4,32,512]{2,1,0:T(8,128)} %get-tuple-element.5.r_hbm), custom_call_target="tpu_custom_call" | custom-call | tf_op jit(solution)/shard_map/pallas_call | solution.py:464

commit v6 on v5

--- a/solution.py
+++ b/solution.py
@@ -371,6 +371,10 @@
             def _():
                 gather_third(tc, step_net)
 
+            @pl.when(in_c)
+            def _():
+                products(tc, 1)
+
             @pl.when(in_b)
             def _():
                 take_step(tb)
@@ -383,9 +387,9 @@
             @pl.when(in_c)
             def _():
                 products(tc, -1)
-                products(tc, 1)
 
             residual(td, side, weight)
+
             return carry
 
         lax.fori_loop(2, rounds + STREAMS + 1, one_pass, 0)

time: 205 us -> 204 us (level)
  no operation moved by 1% of the time
where the time goes in v6:
time: 204 us
  Pallas kernels  203 us (100%)
    pallas_call x1, Pallas kernels, local(): pl.pallas_call(make_kernel(rows * samp_size, tgt), out_shape=(jax.ShapeDt...  198 us
    pallas_call x1, Pallas kernels, local(): pl.pallas_call(flip_results, in_specs=[any_spec, any_spec], out_specs=(an...  4.77 us

profile of v6, /device:TPU:1, one launch (start us, length us, event | category | flops | bytes accessed | tf_op | source)
XLA Modules:
  0.0 203.6 jit_solution(17766217131540308607)
XLA Ops:
  0.6 198.2 %shard_map.68 = (f32[4,4,4,2,32,256]{5,4,3,2,1,0:T(8,128)}, f32[4,32,512]{2,1,0:T(8,128)}) custom-call(bf16[512,8192]{1,0:T(8,128)(2,1)} %x_hbm.1, f32[512,128]{1,0:T(8,128)} %y_hbm.1, f32[32,256,128]{2,1,0:T(8,128)} %bitcast.3, f32[64,128]{1,0:T(8,128)} %bitcast.4, f32[1,128]{1,0:T(1,128)} %bitcast.5), custom_call_target="tpu_custom_call" | custom-call | tf_op jit(solution)/shard_map/pallas_call | solution.py:427
  198.9 4.8 %shard_map.69 = (f32[8192,128]{1,0:T(8,128)}, f32[512,128]{1,0:T(8,128)}) custom-call(f32[4,4,4,2,32,256]{5,4,3,2,1,0:T(8,128)} %get-tuple-element.4.w_hbm, f32[4,32,512]{2,1,0:T(8,128)} %get-tuple-element.5.r_hbm), custom_call_target="tpu_custom_call" | custom-call | tf_op jit(solution)/shard_map/pallas_call | solution.py:468

commit v7 on v6

--- a/solution.py
+++ b/solution.py
@@ -182,13 +182,13 @@
                         res = jnp.dot(rt[t], xv[(zi * RING + yi) * 2 + h], preferred_element_type=F32)
                         gt[t, h, io, 0, js] = res[:, :LANES]
                         gt[t, h, io, 1, js] = res[:, LANES:]
-            for io in ios:
-                for h in range(2):
                     if io == 2:
                         for part in range(2):
                             rs1(t, h, "F", 0, part).start()
                             rs1(t, h, "F", 1, part).start()
-                    elif io:
+            for io in ios:
+                for h in range(2):
+                    if io % 2:
                         rs1(t, h, "D", io // 2, 0).start()
 
         def sum_first(t):

time: 204 us -> 206 us (level)
  no operation moved by 1% of the time
where the time goes in v7:
time: 206 us; the launch traced here: 205 us
  Pallas kernels  205 us (100%)
    pallas_call x1, Pallas kernels, local(): pl.pallas_call(make_kernel(rows * samp_size, tgt), out_shape=(jax.ShapeDt...  200 us
    pallas_call x1, Pallas kernels, local(): pl.pallas_call(flip_results, in_specs=[any_spec, any_spec], out_specs=(an...  4.77 us

profile of v7, /device:TPU:1, one launch (start us, length us, event | category | flops | bytes accessed | tf_op | source)
XLA Modules:
  0.0 205.5 jit_solution(559235658433394509)
XLA Ops:
  0.6 200.1 %shard_map.68 = (f32[4,4,4,2,32,256]{5,4,3,2,1,0:T(8,128)}, f32[4,32,512]{2,1,0:T(8,128)}) custom-call(bf16[512,8192]{1,0:T(8,128)(2,1)} %x_hbm.1, f32[512,128]{1,0:T(8,128)} %y_hbm.1, f32[32,256,128]{2,1,0:T(8,128)} %bitcast.3, f32[64,128]{1,0:T(8,128)} %bitcast.4, f32[1,128]{1,0:T(1,128)} %bitcast.5), custom_call_target="tpu_custom_call" | custom-call | tf_op jit(solution)/shard_map/pallas_call | solution.py:427
  200.7 4.8 %shard_map.69 = (f32[8192,128]{1,0:T(8,128)}, f32[512,128]{1,0:T(8,128)}) custom-call(f32[4,4,4,2,32,256]{5,4,3,2,1,0:T(8,128)} %get-tuple-element.4.w_hbm, f32[4,32,512]{2,1,0:T(8,128)} %get-tuple-element.5.r_hbm), custom_call_target="tpu_custom_call" | custom-call | tf_op jit(solution)/shard_map/pallas_call | solution.py:468
